TPU v7x, 32 devices: a whole 2x2x4 slice. The times are simulated.
32 devices in a mesh: seq: 8 (over y, x, core), head: 4 (over z).
Axes of the slice: x: 2, y: 2, z: 4, core: 2. Of those that a mesh axis runs over, the one named last changes fastest.
Arguments:
- queries: bfloat16 [2048, 16384], P('seq', 'head'), may hold values from -6 to 6
- keys: bfloat16 [2048, 1024], P('seq', 'head'), may hold values from -6 to 6
- values: bfloat16 [2048, 1024], P('seq', 'head'), may hold values from -6 to 6
- teacher: bfloat16 [2048, 16384], P('seq', 'head'), may hold values from -17 to 17
- map_q: bfloat16 [128, 128, 64], P('head'), may hold values from -0.5 to 0.5
- map_k: bfloat16 [128, 128, 64], P('head'), may hold values from -0.5 to 0.5
Outputs:
- grad_map_q: float32 [128, 128, 64], P('head', 'seq')
- grad_map_k: float32 [128, 128, 64], P('head', 'seq')
All inputs are finite; a program needn't handle non-finite values.
Results may differ from a plain program's by a relative error of at most 0.0003.
Values sent between devices are 32-bit elements; how exact they have to be, the bound alone decides.
No kernel may reach another device: no remote copies, remote signals or barrier semaphores. Data moves between devices by JAX's collectives and lax.ppermute only.
A program may use at most 128 MiB of HBM per device.

v0:
```python
import jax
import jax.numpy as jnp
from jax import lax
from jax.sharding import PartitionSpec as P

HEADS = 128
DH = 128
BLOCK = 256


exact_mode = lax.Precision.HIGHEST


def halves(inputs, weight):
    logits = jnp.einsum("nhld,hdf->nhlf", inputs, weight, preferred_element_type=jnp.float32)
    positive = jnp.exp(logits)
    negative = jnp.exp(-logits)
    up_soft = positive / jnp.sum(positive, -1, keepdims=True)
    down_soft = negative / jnp.sum(negative, -1, keepdims=True)
    return (up_soft, down_soft)


def map_grad(inputs, up_soft, down_soft, grad_feat, half_width):
    grad_up = grad_feat[..., :half_width]
    grad_down = grad_feat[..., half_width:]
    grad_logit = up_soft * (grad_up - jnp.sum(up_soft * grad_up, -1, keepdims=True))
    grad_logit = grad_logit - down_soft * (
        grad_down - jnp.sum(down_soft * grad_down, -1, keepdims=True)
    )
    return jnp.einsum(
        "nhld,nhlf->hdf", inputs.astype(jnp.float32), grad_logit, precision=exact_mode
    )


def on_device(queries, keys, values, teacher, map_q, map_k):
    head_count = map_q.shape[0]
    head_width = map_q.shape[1]
    half_width = map_q.shape[2]
    tokens = queries.shape[0]
    block_count = tokens // BLOCK
    shared_count = keys.shape[1] // head_width
    group_size = head_count // shared_count

    def blocked(source, count):
        return source.reshape(block_count, BLOCK, count, head_width).transpose(0, 2, 1, 3)

    query_blk = blocked(queries, head_count)
    key_blk = jnp.repeat(blocked(keys, shared_count), group_size, axis=1)
    value_blk = jnp.repeat(blocked(values, shared_count), group_size, axis=1)
    teacher_blk = blocked(teacher, head_count)
    local_power = jnp.sum(jnp.square(teacher.astype(jnp.float32)), axis=1)
    power = lax.psum(local_power, "head") / (HEADS * DH) + 1e-05
    power_blk = power.reshape(block_count, BLOCK)
    q_up, q_down = halves(query_blk, map_q)
    k_up, k_down = halves(key_blk, map_k)
    query_feat = jnp.concatenate([q_up, q_down], -1)
    key_feat = jnp.concatenate([k_up, k_down], -1)
    local_state = jnp.einsum(
        "nhlf,nhld->hfd", key_feat, value_blk.astype(jnp.float32), precision=exact_mode
    )
    local_total = jnp.sum(key_feat, axis=(0, 2))
    own_index = lax.axis_index("seq")
    pieces = (
        lax.all_gather(local_state[None], "seq", axis=0, tiled=True),
        lax.all_gather(local_total[None], "seq", axis=0, tiled=True),
    )
    row_count = pieces[0].shape[0]
    lower_mask = (jnp.arange(row_count, dtype=jnp.int32) < own_index).astype(jnp.float32)
    state_start = jnp.einsum("r,rhfd->hfd", lower_mask, pieces[0], precision=exact_mode)
    total_start = jnp.einsum("r,rhf->hf", lower_mask, pieces[1], precision=exact_mode)
    causal = jnp.tril(jnp.ones((BLOCK, BLOCK), jnp.float32))

    def forward(carried, blocks):
        kv_state, key_total = carried
        q_cur, k_cur, v_cur, t_cur, p_cur = blocks
        v_float = v_cur.astype(jnp.float32)
        scores = jnp.einsum("hqf,hkf->hqk", q_cur, k_cur, precision=exact_mode) * causal
        numerator = jnp.einsum("hqf,hfd->hqd", q_cur, kv_state, precision=exact_mode)
        numerator = numerator + jnp.einsum("hqk,hkd->hqd", scores, v_float, precision=exact_mode)
        denominator = jnp.einsum("hqf,hf->hq", q_cur, key_total, precision=exact_mode) + jnp.sum(
            scores, -1
        )
        student = numerator / denominator[..., None]
        grad_out = (student - t_cur.astype(jnp.float32)) / p_cur[None, :, None]
        grad_numer = grad_out / denominator[..., None]
        grad_denom = -jnp.sum(grad_out * student, -1) / denominator
        back_scores = (
            jnp.einsum("hqd,hkd->hqk", grad_numer, v_float, precision=exact_mode)
            + grad_denom[..., None]
        ) * causal
        grad_qfeat = jnp.einsum("hfd,hqd->hqf", kv_state, grad_numer, precision=exact_mode)
        grad_qfeat = grad_qfeat + grad_denom[..., None] * key_total[:, None, :]
        grad_qfeat = grad_qfeat + jnp.einsum(
            "hqk,hkf->hqf", back_scores, k_cur, precision=exact_mode
        )
        new_state = kv_state + jnp.einsum("hkf,hkd->hfd", k_cur, v_float, precision=exact_mode)
        return ((new_state, key_total + jnp.sum(k_cur, 1)), (grad_qfeat, grad_numer, grad_denom))

    _, (grad_qfeat, grad_numer, grad_denom) = lax.scan(
        forward,
        (state_start, total_start),
        (query_feat, key_feat, value_blk, teacher_blk, power_blk),
    )
    local_gstate = jnp.einsum("nhlf,nhld->hfd", query_feat, grad_numer, precision=exact_mode)
    local_gtotal = jnp.einsum("nhlf,nhl->hf", query_feat, grad_denom, precision=exact_mode)
    own_place = lax.axis_index("seq")
    pieces = (
        lax.all_gather(local_gstate[None], "seq", axis=0, tiled=True),
        lax.all_gather(local_gtotal[None], "seq", axis=0, tiled=True),
    )
    row_count = pieces[0].shape[0]
    upper_mask = (jnp.arange(row_count, dtype=jnp.int32) > own_place).astype(jnp.float32)
    gstate_end = jnp.einsum("r,rhfd->hfd", upper_mask, pieces[0], precision=exact_mode)
    gtotal_end = jnp.einsum("r,rhf->hf", upper_mask, pieces[1], precision=exact_mode)

    def backward(carried, blocks):
        grad_state, grad_total = carried
        q_cur, k_cur, v_cur, gn_cur, gd_cur = blocks
        v_float = v_cur.astype(jnp.float32)
        back_scores = (
            jnp.einsum("hqd,hkd->hqk", gn_cur, v_float, precision=exact_mode) + gd_cur[..., None]
        ) * causal
        grad_kfeat = jnp.einsum("hqk,hqf->hkf", back_scores, q_cur, precision=exact_mode)
        grad_kfeat = grad_kfeat + jnp.einsum(
            "hfd,hkd->hkf", grad_state, v_float, precision=exact_mode
        )
        grad_kfeat = grad_kfeat + grad_total[:, None, :]
        new_grad = grad_state + jnp.einsum("hqf,hqd->hfd", q_cur, gn_cur, precision=exact_mode)
        new_total = grad_total + jnp.einsum("hqf,hq->hf", q_cur, gd_cur, precision=exact_mode)
        return ((new_grad, new_total), grad_kfeat)

    _, grad_kfeat = lax.scan(
        backward,
        (gstate_end, gtotal_end),
        (query_feat, key_feat, value_blk, grad_numer, grad_denom),
        reverse=True,
    )
    local_gq = map_grad(query_blk, q_up, q_down, grad_qfeat, half_width)
    local_gk = map_grad(key_blk, k_up, k_down, grad_kfeat, half_width)
    grad_map_q, grad_map_k = (
        lax.psum_scatter(local_gq, "seq", scatter_dimension=1, tiled=True),
        lax.psum_scatter(local_gk, "seq", scatter_dimension=1, tiled=True),
    )
    return (grad_map_q, grad_map_k)


def solution(mesh):
    return jax.shard_map(
        on_device,
        mesh=mesh,
        in_specs=(
            P("seq", "head"),
            P("seq", "head"),
            P("seq", "head"),
            P("seq", "head"),
            P("head", None, None),
            P("head", None, None),
        ),
        out_specs=(P("head", "seq", None), P("head", "seq", None)),
        check_vma=False,
    )
```

profile of v0, /device:TPU:0, one launch (start us, length us, event | category | flops | bytes accessed | tf_op | source)
XLA Modules:
  0.0 337.5 jit_solution(6741641425121377161)
XLA Ops:
  13.8 3.7 %fusion.13 = f32[32,128,128]{2,1,0:T(8,128)} fusion(bf16[32,256,128]{2,1,0:T(8,128)(2,1)S(1)} %bitcast.145, f32[1,32,256,64]{2,3,1,0:T(8,128)S(1)} %get-tuple-element.71, f32[1,32,256,64]{2,3,1,0:T(8,128)S(1)} %get-tuple-element.70), kind=kOutput, calls=%fused_computation.18 | convolution fusion | flops 1611661312 | bytes 8388608 | tf_op jit(solution)/shard_map/nhlf,nhld->hfd/dot_general | solution.py:58
  17.5 3.4 copy.72
  20.9 4.3 %copy.35 = f32[256,4096]{0,1:T(8,128)} copy(bf16[256,4096]{1,0:T(8,128)(2,1)} %param.9) | data formatting | bytes 6291456 | tf_op jit(solution)/shard_map/while/body/eval_jaxpr/convert_element_type | solution.py:84
  25.2 2.1 multiply_reduce_fusion.2
  27.3 13.8 %psum.7 = f32[256]{0:T(256)S(1)} all-reduce(f32[256]{0:T(256)S(1)} %multiply_reduce_fusion.2), channel_id=1, replica_groups=mesh['seq'=8,'head'=4] {'head'}, use_global_device_ids=true, to_apply=%region_7.8 | all-reduce | flops 256 | bytes 2048 | tf_op jit(solution)/shard_map/psum | solution.py:52
  41.1 2.4 fusion.41
  43.5 10.2 %all-gather.1 = f32[256,128]{1,0:T(8,128)S(1)} all-gather(f32[32,128]{1,0:T(8,128)S(1)} %fusion.41), channel_id=3, replica_groups=mesh['seq'=8,'head'=4] {'seq'}, dimensions={0}, use_global_device_ids=true | all-gather | bytes 147456 | tf_op jit(solution)/shard_map/all_gather | solution.py:65
  56.2 2.3 fusion.58
  59.2 19.0 %multiply_reduce_fusion = (f32[32,256]{1,0:T(8,128)S(1)}, f32[32,256,256]{1,2,0:T(8,128)S(1)}) fusion(f32[256,256]{0,1:T(8,128)S(1)} %fusion.59, f32[1,32,256,64]{2,3,1,0:T(8,128)S(1)} %copy-done.11, f32[1,32,256,64]{2,3,1,0:T(8,128)S(1)} %copy-done.7, f32[1,32,256,64]{2,3,1,0:T(8,128)S(1)} %get-tuple-element.73, f32[1,32,256,64]{2,3,1,0:T(8,128)S(1)} %get-tuple-element.72), kind=kOutput, calls=%fused_computation.5 | convolution fusion | flops 3227508736 | bytes 17072128 | tf_op jit(solution)/shard_map/while/body/eval_jaxpr/hqf,hkf->hqk/dot_general | solution.py:77
  78.2 6.3 %fusion.4 = f32[32,256,128]{1,2,0:T(8,128)} fusion(bf16[32,256,128]{2,1,0:T(8,128)(2,1)S(1)} %bitcast.147, f32[32,256,256]{1,2,0:T(8,128)S(1)} %get-tuple-element.86, f32[256,256]{0,1:T(8,128)S(1)} %fusion.59), kind=kOutput, calls=%fused_computation.6 | convolution fusion | flops 3223322624 | bytes 14942208 | tf_op jit(solution)/shard_map/while/body/eval_jaxpr/hqk,hkd->hqd/dot_general | solution.py:79
  84.6 26.0 %all-gather.7.cloned.1.call-done = f32[256,128,128]{2,1,0:T(8,128)} async-done(((f32[32,128,128]{2,1,0:T(8,128)}), f32[256,128,128]{2,1,0:T(8,128)}) %all-gather.7.cloned.1.call-update) | async-done | bytes 16777232 | tf_op jit(solution)/shard_map/all_gather | solution.py:64
  110.6 22.4 %fusion.2 = f32[1,32,128,128]{3,0,2,1:T(1,128)S(1)} fusion(f32[8,32,128,128]{3,2,1,0:T(8,128)} %bitcast.151, s32[]{:T(128)S(6)} %axis_index.19), kind=kOutput, calls=%fused_computation.2 | convolution fusion | flops 50331656 | bytes 18874372 | tf_op jit(solution)/shard_map/r,rhfd->hfd/dot_general | solution.py:69
  133.0 9.4 %multiply_reduce_fusion.1 = (f32[32,256]{1,0:T(8,128)S(1)}, f32[32,256,128]{1,2,0:T(8,128)S(1)}) fusion(f32[256]{0:T(256)S(1)} %multiply_add_fusion, f32[256,4096]{0,1:T(8,128)} %copy.35, f32[32,256]{1,0:T(8,128)S(1)} %bitcast_add_fusion.1, f32[32,256,128]{1,2,0:T(8,128)} %bitcast.158, f32[32,256,128]{1,2,0:T(8,128)S(1)} %copy-done.25, ...), kind=kOutput, calls=%fused_computation.23 | convolution fusion | flops 1621090304 | bytes 23135232 | tf_op jit(solution)/shard_map/while/body/eval_jaxpr/hqf,hfd->hqd/dot_general | solution.py:78
  142.4 1.9 copy-done.18
  144.4 5.4 %fusion.57 = f32[32,128,128]{2,1,0:T(8,128)} fusion(f32[32,256,128]{1,2,0:T(8,128)S(1)} %get-tuple-element.69, f32[1,32,256,64]{2,3,1,0:T(8,128)S(1)} %copy-done.3, f32[1,32,256,64]{2,3,1,0:T(8,128)S(1)} %get-tuple-element.72), kind=kOutput, calls=%fused_computation.75 | convolution fusion | flops 1611661312 | bytes 10485760 | tf_op jit(solution)/shard_map/nhlf,nhld->hfd/dot_general | solution.py:104
  149.9 7.3 %fusion.90 = f32[32,256,256]{1,2,0:T(8,128)S(1)} fusion(f32[32,256,128]{1,2,0:T(8,128)} %copy-done.18, bf16[32,256,128]{2,1,0:T(8,128)(2,1)} %bitcast.146), kind=kOutput, calls=%fused_computation.112 | convolution fusion | flops 3221225472 | bytes 14680064 | tf_op jit(solution)/shard_map/while/body/eval_jaxpr/hqd,hkd->hqk/dot_general | solution.py:88
  157.3 7.7 %fusion.7 = f32[32,256,128]{1,2,0:T(8,128)} fusion(f32[32,256,256]{1,2,0:T(8,128)S(1)} %fusion.90, f32[32,256]{1,0:T(8,128)S(1)} %negate_divide_fusion, f32[256,256]{0,1:T(8,128)S(1)} %fusion.59, f32[1,32,256,64]{2,3,1,0:T(8,128)S(1)} %copy-done.12, f32[1,32,256,64]{2,3,1,0:T(8,128)S(1)} %copy-done.8), kind=kOutput, calls=%fused_computation.9 | convolution fusion | flops 3226468352 | bytes 17072128 | tf_op jit(solution)/shard_map/while/body/eval_jaxpr/hqk,hkf->hqf/dot_general | solution.py:93
  165.0 9.0 %add_bitcast_fusion = f32[1,32,256,128]{2,3,1,0:T(8,128)S(1)} fusion(f32[32,256,128]{1,2,0:T(8,128)} %fusion.7, f32[32,256,128]{1,2,0:T(8,128)} %copy-done.18, f32[32,128,128]{2,1,0:T(8,128)} %bitcast.156, f32[32,128]{1,0:T(8,128)S(1)} %bitcast.165, f32[32,256]{1,0:T(8,128)S(1)} %negate_divide_fusion), kind=kOutput, calls=%fused_computation.20 | convolution fusion | flops 1613758464 | bytes 14729216 | tf_op jit(solution)/shard_map/while/body/eval_jaxpr/hfd,hqd->hqf/dot_general | solution.py:91
  175.6 3.6 %fusion.47 = f32[32,128,64]{1,2,0:T(8,128)} fusion(bf16[1,256,32,128]{3,2,1,0:T(8,128)(2,1)S(1)} %bitcast.154, f32[1,32,256,64]{2,3,1,0:T(8,128)S(1)} %copy-done.4, f32[1,32,256,64]{2,3,1,0:T(8,128)S(1)} %get-tuple-element.72, f32[1,32,256,128]{2,3,1,0:T(8,128)S(1)} %add_bitcast_fusion, f32[32,256]{1,0:T(8,128)S(1)} %get-tuple-element.54, ...), kind=kOutput, calls=%fused_computation.69 | convolution fusion | flops 807927808 | bytes 11599872 | tf_op jit(solution)/shard_map/nhld,nhlf->hdf/dot_general | solution.py:30
  179.1 4.1 %copy.40 = f32[32,128,64]{2,0,1:T(8,128)} copy(f32[32,128,64]{1,2,0:T(8,128)} %fusion.47) | data formatting | bytes 2097152 | tf_op jit(solution)/shard_map/nhld,nhlf->hdf/dot_general | solution.py:30
  183.2 5.5 %fusion.56 = f32[32,1,128]{2,1,0:T(1,128)S(1)} fusion(f32[1,32,256,64]{2,3,1,0:T(8,128)} %copy-done.2, f32[1,32,256,64]{2,3,1,0:T(8,128)S(1)} %get-tuple-element.72, f32[32,256,1]{1,0,2:T(8,128)S(1)} %bitcast.160), kind=kOutput, calls=%fused_computation.74 | convolution fusion | flops 13631488 | bytes 4243456 | tf_op jit(solution)/shard_map/nhlf,nhl->hf/dot_general | solution.py:105
  188.7 9.8 %all-gather.3 = f32[256,128]{1,0:T(8,128)S(1)} all-gather(f32[32,128]{1,0:T(8,128)S(1)} %bitcast.167), channel_id=5, replica_groups=mesh['seq'=8,'head'=4] {'seq'}, dimensions={0}, use_global_device_ids=true | all-gather | bytes 147456 | tf_op jit(solution)/shard_map/all_gather | solution.py:109
  198.8 15.0 %fusion.6 = f32[32,256,128]{1,2,0:T(8,128)} fusion(f32[32,256,256]{1,2,0:T(8,128)} %copy-done.14, f32[32,256]{1,0:T(8,128)S(1)} %negate_divide_fusion, f32[256,256]{0,1:T(8,128)S(1)} %fusion.59, f32[1,32,256,64]{2,3,1,0:T(8,128)S(1)} %copy-done.5, f32[1,32,256,64]{2,3,1,0:T(8,128)S(1)} %get-tuple-element.72), kind=kOutput, calls=%fused_computation.8 | convolution fusion | flops 3226468352 | bytes 17072128 | tf_op jit(solution)/shard_map/while/body/eval_jaxpr/hqk,hqf->hkf/dot_general | solution.py:123
  213.8 26.4 %all-gather.9.cloned.1.call-done = f32[256,128,128]{2,1,0:T(8,128)} async-done(((f32[32,128,128]{2,1,0:T(8,128)}), f32[256,128,128]{2,1,0:T(8,128)}) %all-gather.9.cloned.1.call-update) | async-done | bytes 16777232 | tf_op jit(solution)/shard_map/all_gather | solution.py:108
  240.2 22.8 %fusion = f32[1,32,128,128]{3,0,2,1:T(1,128)S(1)} fusion(f32[8,32,128,128]{3,2,1,0:T(8,128)} %bitcast.152, s32[]{:T(128)S(6)} %axis_index.19), kind=kOutput, calls=%fused_computation | convolution fusion | flops 50331656 | bytes 18874372 | tf_op jit(solution)/shard_map/r,rhfd->hfd/dot_general | solution.py:113
  263.1 2.6 fusion.9
  267.3 1.7 fusion.44
  269.1 2.8 copy.43
  271.9 12.8 %reduce-scatter.3.cloned.1.call-done = f32[32,16,64]{2,0,1:T(8,128)} async-done(((f32[32,128,64]{2,0,1:T(8,128)}), f32[32,16,64]{2,0,1:T(8,128)}) %reduce-scatter.3.cloned.1.call-update) | async-done | bytes 131088 | tf_op jit(solution)/shard_map/reduce_scatter | solution.py:141
  284.7 1.8 copy.44
  286.5 42.5 %reduce-scatter.5.cloned.1.call-done = f32[32,16,64]{2,0,1:T(8,128)} async-done(((f32[32,128,64]{2,0,1:T(8,128)}), f32[32,16,64]{2,0,1:T(8,128)}) %reduce-scatter.5.cloned.1.call-update) | async-done | bytes 131088 | tf_op jit(solution)/shard_map/reduce_scatter | solution.py:142
  328.9 1.8 copy.45
  (79 shorter events, 13.3 us)
Async XLA Ops:
  7.2 2.5 copy-start
  7.2 103.4 %all-gather.7.cloned.1.call-start = ((), (), s32[]{:S(2)}) async-start(), calls=%async_computation.4 | async-start | bytes 18874368 | tf_op jit(solution)/shard_map/all_gather | solution.py:64
  9.7 1.3 copy-start.19
  11.7 1.4 copy-start.10
  11.7 29.4 %copy-start.6 = (f32[1,32,256,64]{2,3,1,0:T(8,128)}, f32[1,32,256,64]{2,3,1,0:T(8,128)S(1)}, u32[]{:S(2)}) copy-start(f32[1,32,256,64]{2,3,1,0:T(8,128)S(1)} %get-tuple-element.70) | copy-start | bytes 6291460
  12.1 1.6 copy-start.15
  17.5 222.8 %all-gather.9.cloned.1.call-start = ((), (), s32[]{:S(2)}) async-start(), calls=%async_computation.5 | async-start | bytes 18874368 | tf_op jit(solution)/shard_map/all_gather | solution.py:108
  41.1 12.9 %copy-start.22 = (bf16[32,8,32,128]{3,2,1,0:T(8,128)(2,1)S(1)}, bf16[32,8,32,128]{3,2,1,0:T(8,128)(2,1)}, u32[]{:S(2)}) copy-start(bf16[32,8,32,128]{3,2,1,0:T(8,128)(2,1)} %copy.72) | copy-start | bytes 6291460
  41.1 12.9 %copy-start.26 = (bf16[32,128,64]{1,2,0:T(8,128)(2,1)S(1)}, bf16[32,128,64]{1,2,0:T(8,128)(2,1)}, u32[]{:S(2)}) copy-start(bf16[32,128,64]{1,2,0:T(8,128)(2,1)} %param.10) | copy-start | bytes 1572868
  56.2 2.3 copy-start.2
  56.2 2.3 copy-start.7
  56.2 3.0 copy-start.11
  59.2 19.0 %copy-start.16 = (bf16[2,16,256,128]{3,2,1,0:T(8,128)(2,1)S(1)}, bf16[2,16,256,128]{3,2,1,0:T(8,128)(2,1)}, u32[]{:S(2)}) copy-start(bf16[2,16,256,128]{3,2,1,0:T(8,128)(2,1)} %copy-done.15) | copy-start | bytes 6291460
  110.6 22.4 %copy-start.3 = (f32[1,32,256,64]{2,3,1,0:T(8,128)S(1)}, f32[1,32,256,64]{2,3,1,0:T(8,128)}, u32[]{:S(2)}) copy-start(f32[1,32,256,64]{2,3,1,0:T(8,128)} %copy-done.2) | copy-start | bytes 6291460
  110.6 22.4 %copy-start.25 = (f32[32,256,128]{1,2,0:T(8,128)S(1)}, f32[32,256,128]{1,2,0:T(8,128)}, u32[]{:S(2)}) copy-start(f32[32,256,128]{1,2,0:T(8,128)} %fusion.4) | copy-start | bytes 12582916
  133.0 9.5 %copy-start.24 = (f32[1,32,128,128]{3,0,2,1:T(1,128)}, f32[1,32,128,128]{3,0,2,1:T(1,128)S(1)}, u32[]{:S(2)}) copy-start(f32[1,32,128,128]{3,0,2,1:T(1,128)S(1)} %fusion.2) | copy-start | bytes 6291460
  142.4 2.0 copy-start.18
  149.8 134.8 %reduce-scatter.3.cloned.1.call-start = ((), (), s32[]{:S(2)}) async-start(), calls=%async_computation.2 | async-start | bytes 2359296 | tf_op jit(solution)/shard_map/reduce_scatter | solution.py:141
  149.9 7.3 %copy-start.8 = (f32[1,32,256,64]{2,3,1,0:T(8,128)S(1)}, f32[1,32,256,64]{2,3,1,0:T(8,128)}, u32[]{:S(2)}) copy-start(f32[1,32,256,64]{2,3,1,0:T(8,128)} %copy-done.6) | copy-start | bytes 6291460
  149.9 7.3 %copy-start.12 = (f32[1,32,256,64]{2,3,1,0:T(8,128)S(1)}, f32[1,32,256,64]{2,3,1,0:T(8,128)}, u32[]{:S(2)}) copy-start(f32[1,32,256,64]{2,3,1,0:T(8,128)} %copy-done.10) | copy-start | bytes 6291460
  157.3 7.7 %copy-start.14 = (f32[32,256,256]{1,2,0:T(8,128)}, f32[32,256,256]{1,2,0:T(8,128)S(1)}, u32[]{:S(2)}) copy-start(f32[32,256,256]{1,2,0:T(8,128)S(1)} %fusion.90) | copy-start | bytes 25165828
  164.9 9.0 %copy-start.4 = (f32[1,32,256,64]{2,3,1,0:T(8,128)S(1)}, f32[1,32,256,64]{2,3,1,0:T(8,128)}, u32[]{:S(2)}) copy-start(f32[1,32,256,64]{2,3,1,0:T(8,128)} %copy-done.2) | copy-start | bytes 6291460
  174.0 1.6 copy-start.23
  183.2 15.6 %copy-start.5 = (f32[1,32,256,64]{2,3,1,0:T(8,128)S(1)}, f32[1,32,256,64]{2,3,1,0:T(8,128)}, u32[]{:S(2)}) copy-start(f32[1,32,256,64]{2,3,1,0:T(8,128)} %copy-done.2) | copy-start | bytes 6291460
  213.8 115.2 %reduce-scatter.5.cloned.1.call-start = ((), (), s32[]{:S(2)}) async-start(), calls=%async_computation.3 | async-start | bytes 2359296 | tf_op jit(solution)/shard_map/reduce_scatter | solution.py:142
  240.2 22.8 %copy-start.17 = (bf16[2,16,256,128]{3,2,1,0:T(8,128)(2,1)S(1)}, bf16[2,16,256,128]{3,2,1,0:T(8,128)(2,1)}, u32[]{:S(2)}) copy-start(bf16[2,16,256,128]{3,2,1,0:T(8,128)(2,1)} %copy-done.15) | copy-start | bytes 6291460
  240.2 22.8 %copy-start.21 = (f32[32,256,128]{1,2,0:T(8,128)S(1)}, f32[32,256,128]{1,2,0:T(8,128)}, u32[]{:S(2)}) copy-start(f32[32,256,128]{1,2,0:T(8,128)} %fusion.6) | copy-start | bytes 12582916
  263.1 2.6 copy-start.9
  263.1 2.6 copy-start.13
  265.7 1.6 copy-start.20
  269.0 61.7 %copy-start.1 = (bf16[32,128,64]{1,2,0:T(8,128)(2,1)S(1)}, bf16[32,128,64]{1,2,0:T(8,128)(2,1)}, u32[]{:S(2)}) copy-start(bf16[32,128,64]{1,2,0:T(8,128)(2,1)} %param.11) | copy-start | bytes 1572868
Sparse Core Ops, SparseCore 0:
  17.6 92.9 all-gather.6
  150.0 90.2 all-gather.8
  243.5 41.0 reduce-scatter.2
  287.8 41.0 reduce-scatter.4
where the time goes:
time: 343 us; the launch traced here: 337 us
  matrix products  147 us (43%)
  waiting for transfers between devices  108 us (31%)
  blocking collectives  33.8 us (10%)
  local copies, waits for them, and re-layouts  26.5 us (8%)
  between operations  14.4 us (4%)
  other arithmetic  8.19 us (2%)
    reduce_scatter x1, waiting for transfers between devices, on_device(): lax.psum_scatter(local_gk, 'seq', scatter_dimension=1, tiled=True)  42.5 us
    all_gather x1, waiting for transfers between devices, on_device(): lax.all_gather(local_gstate[None], 'seq', axis=0, tiled=True)  26.4 us
    all_gather x1, waiting for transfers between devices, on_device(): lax.all_gather(local_state[None], 'seq', axis=0, tiled=True)  26 us
    dot_general x1, matrix products, on_device(): jnp.einsum('r,rhfd->hfd', upper_mask, pieces[0], precision=exact_mode)  22.8 us
    dot_general x1, matrix products, on_device(): jnp.einsum('r,rhfd->hfd', lower_mask, pieces[0], precision=exact_mode)  22.4 us
    dot_general x1, matrix products, forward(): jnp.einsum('hqf,hkf->hqk', q_cur, k_cur, precision=exact_mode) * causal  19 us
    dot_general x1, matrix products, backward(): jnp.einsum('hqk,hqf->hkf', back_scores, q_cur, precision=exact_mode)  15 us
    psum x1, blocking collectives, on_device(): power = lax.psum(local_power, 'head') / (HEADS * DH) + 1e-05  13.8 us
  transfers between devices with their start and end apart: 4, of which 4 were waited for; matrix products, arithmetic and copies ran while one was open for 38% of the time, Pallas kernels for 0%

commit v1 on v0

v1 whole, which is shorter than its diff:
```python
import functools

import jax
import jax.numpy as jnp
from jax import lax
from jax.experimental import pallas as pl
from jax.experimental.pallas import tpu as pltpu
from jax.sharding import PartitionSpec as P

F32, BF16 = jnp.float32, jnp.bfloat16
LANES = 128
ROWS = 16
STEP_A = 2
STEP_B = 4
PARTS = (1, 1)
VMEM_LIMIT = 60 * 1024 * 1024


def split(x):
    high = x.astype(BF16)
    return high, (x - high.astype(F32)).astype(BF16)


def mm(a, b):
    return jnp.dot(a, b, preferred_element_type=F32)


def mm_nt(a, b):
    return lax.dot_general(a, b, (((1,), (1,)), ((), ())), preferred_element_type=F32)


def cat(parts, axis):
    return jnp.concatenate(parts, axis)


def features(logits):
    up, down = jnp.exp(logits), jnp.exp(-logits)
    up = up * (1.0 / jnp.sum(up, 0, keepdims=True))
    down = down * (1.0 / jnp.sum(down, 0, keepdims=True))
    return cat([up, down], 0)


def features_back(feat, grad):
    half = feat.shape[0] // 2
    prod = feat * grad
    up, down = prod[:half], prod[half:]
    up = up - feat[:half] * jnp.sum(up, 0, keepdims=True)
    down = down - feat[half:] * jnp.sum(down, 0, keepdims=True)
    return up - down


def causal_mask(size):
    row = lax.broadcasted_iota(jnp.int32, (size, size), 0)
    col = lax.broadcasted_iota(jnp.int32, (size, size), 1)
    return row <= col


def with_ones(v):
    return cat([v, jnp.ones_like(v)], 1)


def local_kernel(pair, block, width, half, pos_ref, *refs):
    refs = list(refs)
    q_own = refs.pop(0)
    q_got = refs.pop(0) if pair > 1 else None
    wq, wk, kv = refs[:3]
    q_out, qh_out, ql_out, kh_out, kl_out, num_out, state_out = refs[3:10]
    k_nat, v_aug, v_tr = refs[10:]
    heads = wq.shape[0]
    tokens = pair * block

    @pl.when(pl.program_id(0) == 0)
    def _():
        k_nat[...] = kv[:, :width].astype(BF16)
        v = kv[:, width:]
        v_aug[...] = with_ones(v).astype(BF16)
        v_tr[:width] = v.T.astype(BF16)
        v_tr[width:] = jnp.ones((ROWS, tokens), BF16)

    mask = causal_mask(block)
    k_logits = mm_nt(wk[...].reshape(heads * half, width), k_nat[...])
    for h in range(heads):
        cols = slice(h * width, (h + 1) * width)
        if pair > 1:
            place = pos_ref[0]
            q_out[h, pl.ds(pl.multiple_of(place * block, block), block)] = q_own[:, cols]
            q_out[h, pl.ds(pl.multiple_of((1 - place) * block, block), block)] = q_got[
                :, cols
            ].astype(BF16)
        else:
            q_out[h] = q_own[:, cols]
        qh, ql = split(features(mm_nt(wq[h], q_out[h])))
        kh, kl = split(features(k_logits[h * half : (h + 1) * half]))
        qh_out[h] = qh
        ql_out[h] = ql
        kh_out[h] = kh
        kl_out[h] = kl
        for b in range(pair):
            at = slice(b * block, (b + 1) * block)
            kth, ktl = kh[:, at].T, kl[:, at].T
            scores = mm(cat([kth, kth, ktl], 1), cat([qh[:, at], ql[:, at], qh[:, at]], 0))
            sh, sl = split(jnp.where(mask, scores, 0.0))
            vt = v_tr[:, at]
            num_out[h, b] = mm(cat([vt, vt], 1), cat([sh, sl], 0))
        if pair > 1:
            va = v_aug[:block]
            state_out[h] = mm(cat([kh[:, :block], kl[:, :block]], 1), cat([va, va], 0))
        else:
            state_out[h] = jnp.zeros(state_out.shape[1:], F32)


def global_kernel(pair, units, block, width, half, pos_ref, *refs):
    refs = list(refs)
    q, qh_in, ql_in, kh_in, kl_in, num_in, state_in, wk, t_own = refs[:9]
    refs = refs[9:]
    t_got = refs.pop(0) if pair > 1 else None
    inv_power, kv = refs[:2]
    out = refs[2]
    k_nat, v_aug, v_tr, feat_old, state, grad_high, grad_low, grad_k, gsum = refs[3:]
    heads = wk.shape[0]
    tokens = pair * block
    place, unit = pos_ref[0], pos_ref[1]

    @pl.when(pl.program_id(0) == 0)
    def _():
        for o in range(units):
            k_nat[o] = kv[o, :, :width].astype(BF16)
            v = kv[o, :, width:]
            v_aug[o] = with_ones(v).astype(BF16)
            v_tr[o, :width] = v.T.astype(BF16)
            v_tr[o, width:] = jnp.ones((width, tokens), BF16)
        grad_high[...] = jnp.zeros_like(grad_high)
        grad_low[...] = jnp.zeros_like(grad_low)

    wk_all = wk[...].reshape(heads * half, width)
    state[...] = jnp.zeros_like(state)

    def ahead(u, carry):
        o = unit ^ u
        logits = mm_nt(wk_all, k_nat[o])
        highs, lows = [], []
        for h in range(heads):
            feat = features(logits[h * half : (h + 1) * half])
            feat_old[u, h] = feat
            fh, fl = split(feat)
            highs.append(fh)
            lows.append(fl)
        va = v_aug[o]
        state[...] += mm(cat([cat(highs, 0), cat(lows, 0)], 1), cat([va, va], 0))
        return carry

    lax.fori_loop(0, unit, ahead, 0)

    mask = causal_mask(block)
    for h in range(heads):
        total_state = state[h * 2 * half : (h + 1) * 2 * half]
        grad_q = jnp.zeros((half, width), F32)
        sums = []
        key_grads = []
        for b in range(pair):
            at = slice(b * block, (b + 1) * block)
            if b == 1:
                total_state = total_state + state_in[h]
            sth, stl = split(total_state)
            turned = total_state.T[: width + ROWS]
            tth, ttl = split(turned)
            qh, ql = qh_in[h, :, at], ql_in[h, :, at]
            kh, kl = kh_in[h, :, at], kl_in[h, :, at]
            numer = num_in[h, b] + mm(cat([tth, tth, ttl], 1), cat([qh, ql, qh], 0))
            inv = 1.0 / numer[width : width + 1]
            student = numer[:width] * inv
            own_t = t_own[:, h * width : (h + 1) * width].astype(F32)
            if pair > 1:
                own_t = jnp.where(place == b, own_t, t_got[:, h * width : (h + 1) * width])
            grad_out = (student - own_t.T) * inv_power[0:1, at]
            gnum = grad_out * inv
            gden = -jnp.sum(grad_out * student, 0, keepdims=True) * inv
            top = lax.broadcasted_iota(jnp.int32, (ROWS, block), 0) == 0
            gh, gl = split(gnum)
            dh, dl = split(jnp.where(top, gden, 0.0))
            grad_high[:width] = gh
            grad_low[:width] = gl
            grad_high[width : width + ROWS] = dh
            grad_low[width : width + ROWS] = dl
            gah, gal = grad_high[...], grad_low[...]
            va = v_aug[0, at]
            back = mm(cat([va, va], 1), cat([gah, gal], 0))
            bh, bl = split(jnp.where(mask, back, 0.0))
            gq = mm(cat([sth, sth, stl], 1), cat([gah, gal, gah], 0)) + mm(
                cat([kh, kh, kl], 1), cat([bh, bl, bh], 0)
            )
            q_feat = qh.astype(F32) + ql.astype(F32)
            lh, ll = split(features_back(q_feat, gq))
            q_nat = q[h, at]
            grad_q = grad_q + mm(cat([lh, ll], 1), cat([q_nat, q_nat], 0))
            small_h, small_l = gah[: width + ROWS], gal[: width + ROWS]
            sums.append(
                mm_nt(cat([small_h, small_h, small_l], 1), cat([qh, ql, qh], 1))
            )
            key_grads.append(mm_nt(cat([qh, qh, ql], 1), cat([bh, bl, bh], 1)))
        grad_kk = jnp.zeros((half, width), F32)
        later = None
        for b in reversed(range(pair)):
            at = slice(b * block, (b + 1) * block)
            gk = key_grads[b]
            if later is not None:
                padded = cat([later, jnp.zeros((width - ROWS, width), F32)], 0).T
                ph, pl_ = split(padded)
                vt = v_tr[0, :, at]
                gk = gk + mm(cat([ph, pl_], 1), cat([vt, vt], 0))
            kh, kl = kh_in[h, :, at], kl_in[h, :, at]
            k_feat = kh.astype(F32) + kl.astype(F32)
            lh, ll = split(features_back(k_feat, gk))
            k_blk = k_nat[0, at]
            grad_kk = grad_kk + mm(cat([lh, ll], 1), cat([k_blk, k_blk], 0))
            later = sums[b] if later is None else later + sums[b]
        padded = cat([later, jnp.zeros((width - ROWS, width), F32)], 0).T
        gsum[h * 2 * half : (h + 1) * 2 * half] = padded
        grad_k[h, :half] = grad_q
        grad_k[h, half:] = grad_kk

    gsh, gsl = split(gsum[...])
    both = cat([gsh, gsl], 1)

    def behind(u, carry):
        o = unit ^ u
        vt = v_tr[o]
        gk = mm(both, cat([vt, vt], 0))
        highs, lows = [], []
        for h in range(heads):
            lh, ll = split(
                features_back(feat_old[u, h], gk[h * 2 * half : (h + 1) * 2 * half])
            )
            highs.append(lh)
            lows.append(ll)
        k_blk = k_nat[o]
        add = mm(cat([cat(highs, 0), cat(lows, 0)], 1), cat([k_blk, k_blk], 0))
        for h in range(heads):
            grad_k[h, half:] += add[h * half : (h + 1) * half]
        return carry

    lax.fori_loop(0, unit, behind, 0)

    share = width // (units * pair)
    for h in range(heads):
        flat = grad_k[h].T
        for u in range(units):
            for r in range(pair):
                slot = (unit ^ u) * pair + (place ^ r)
                start = pl.multiple_of(slot * share, share)
                n = u * pair + r
                out[h, pl.ds(start, share)] = flat[n * share : (n + 1) * share]


def on_device(axis_sizes, queries, keys, values, teacher, map_q, map_k):
    seq_count, head_axis = axis_sizes
    head_count, width, half = map_q.shape
    block = queries.shape[0]
    shared = keys.shape[1] // width
    pair = 2 if shared == 2 and seq_count % 2 == 0 else 1
    units = seq_count // pair
    heads = head_count // pair
    tokens = pair * block
    bits = units.bit_length() - 1
    own = lax.axis_index("seq")
    place, unit = own % pair, own // pair
    pos = jnp.stack([place, unit]).astype(jnp.int32)
    columns = heads * width

    def swap(x, bit):
        return lax.ppermute(x, "seq", [(i, i ^ bit) for i in range(seq_count)])

    def mine(x, size, index):
        return lax.dynamic_slice_in_dim(x, index * size, size, 1)

    def tie(*values):
        return lax.optimization_barrier(values)

    kv = cat([mine(keys, width, place), mine(values, width, place)], 1).astype(F32)
    count = len(PARTS)
    sizes = [heads * n // sum(PARTS) for n in PARTS]
    begins = [sum(sizes[:i]) for i in range(count)]
    first = place == 0
    q_got, t_got = [None] * count, [None] * count
    if pair > 1:
        other = 1 - place
        kv_away = cat([mine(keys, width, other), mine(values, width, other)], 1).astype(F32)
        q_src, kv_away = tie(queries, kv_away)
        kv_got = swap(kv_away, 1)

        def away(source, i):
            start = other * columns + begins[i] * width
            return lax.dynamic_slice_in_dim(source, start, sizes[i] * width, 1).astype(F32)

        q_away = [away(q_src, i) for i in range(count)]
        q_got = [swap(x, 1) for x in q_away]
        t_src, q_last = tie(teacher, q_away[-1])
        t_got = [swap(away(t_src, i), 1) for i in range(count)]
        pieces = [jnp.where(first, kv, kv_got), jnp.where(first, kv_got, kv)]
    else:
        pieces = [kv]
    kv_unit = cat(pieces, 0)

    squares = jnp.sum(jnp.square(teacher.astype(F32)), axis=1)[None]
    others = [
        lax.ppermute(squares, "head", [(i, (i + s) % head_axis) for i in range(head_axis)])
        for s in range(1, head_axis)
    ]

    wq_t, wk_t = jnp.swapaxes(map_q, 1, 2), jnp.swapaxes(map_k, 1, 2)
    two = 2 * half
    whole2 = lambda g, p: (0, 0)
    per_head3 = lambda g, p: (g, 0, 0)
    per_head4 = lambda g, p: (g, 0, 0, 0)
    spec = pl.BlockSpec

    def run_local(i):
        n = min(STEP_A, sizes[i])
        steps = sizes[i] // n
        index = lambda g, p: p[0] * (heads // n) + begins[i] // n + g
        ins = [queries] + ([q_got[i]] if pair > 1 else []) + [wq_t, wk_t, kv_unit]
        in_specs = [spec((block, n * width), lambda g, p: (0, index(g, p)))]
        if pair > 1:
            in_specs.append(spec((block, n * width), lambda g, p: (0, g)))
        in_specs += [spec((n, half, width), lambda g, p: (index(g, p), 0, 0))] * 2
        in_specs.append(spec((tokens, 2 * width), whole2))
        feat_shape = jax.ShapeDtypeStruct((sizes[i], two, tokens), BF16)
        outs = [jax.ShapeDtypeStruct((sizes[i], tokens, width), BF16)] + [feat_shape] * 4
        outs += [
            jax.ShapeDtypeStruct((sizes[i], pair, width + ROWS, block), F32),
            jax.ShapeDtypeStruct((sizes[i], two, 2 * width), F32),
        ]
        out_specs = [spec((n, tokens, width), per_head3)] + [spec((n, two, tokens), per_head3)] * 4
        out_specs += [
            spec((n, pair, width + ROWS, block), per_head4),
            spec((n, two, 2 * width), per_head3),
        ]
        return pl.pallas_call(
            functools.partial(local_kernel, pair, block, width, half),
            out_shape=outs,
            grid_spec=pltpu.PrefetchScalarGridSpec(
                num_scalar_prefetch=1,
                grid=(steps,),
                in_specs=in_specs,
                out_specs=out_specs,
                scratch_shapes=[
                    pltpu.VMEM((tokens, width), BF16),
                    pltpu.VMEM((tokens, 2 * width), BF16),
                    pltpu.VMEM((width + ROWS, tokens), BF16),
                ],
            ),
            compiler_params=pltpu.CompilerParams(
                dimension_semantics=("arbitrary",), vmem_limit_bytes=VMEM_LIMIT
            ),
            cost_estimate=pl.CostEstimate(
                flops=sizes[i] * tokens * 1_500_000, bytes_accessed=10_000_000, transcendentals=0
            ),
            name="local_part",
        )(pos, *ins)

    def run_global(i, local, kv_all, inv_power):
        n = min(STEP_B, sizes[i])
        steps = sizes[i] // n
        index = lambda g, p: p[0] * (heads // n) + begins[i] // n + g
        ins = [*local, wk_t, teacher]
        in_specs = [spec((n, tokens, width), per_head3)] + [spec((n, two, tokens), per_head3)] * 4
        in_specs += [
            spec((n, pair, width + ROWS, block), per_head4),
            spec((n, two, 2 * width), per_head3),
            spec((n, half, width), lambda g, p: (index(g, p), 0, 0)),
            spec((block, n * width), lambda g, p: (0, index(g, p))),
        ]
        if pair > 1:
            ins.append(t_got[i])
            in_specs.append(spec((block, n * width), lambda g, p: (0, g)))
        ins += [inv_power, kv_all]
        in_specs += [
            spec((1, tokens), whole2),
            spec((units, tokens, 2 * width), lambda g, p: (0, 0, 0)),
        ]
        return pl.pallas_call(
            functools.partial(global_kernel, pair, units, block, width, half),
            out_shape=jax.ShapeDtypeStruct((sizes[i], width, two), F32),
            grid_spec=pltpu.PrefetchScalarGridSpec(
                num_scalar_prefetch=1,
                grid=(steps,),
                in_specs=in_specs,
                out_specs=spec((n, width, two), per_head3),
                scratch_shapes=[
                    pltpu.VMEM((units, tokens, width), BF16),
                    pltpu.VMEM((units, tokens, 2 * width), BF16),
                    pltpu.VMEM((units, 2 * width, tokens), BF16),
                    pltpu.VMEM((max(units - 1, 1), n, two, tokens), F32),
                    pltpu.VMEM((n * two, 2 * width), F32),
                    pltpu.VMEM((2 * width, block), BF16),
                    pltpu.VMEM((2 * width, block), BF16),
                    pltpu.VMEM((n, two, width), F32),
                    pltpu.VMEM((n * two, 2 * width), F32),
                ],
            ),
            compiler_params=pltpu.CompilerParams(
                dimension_semantics=("arbitrary",), vmem_limit_bytes=VMEM_LIMIT
            ),
            cost_estimate=pl.CostEstimate(
                flops=sizes[i] * tokens * 3_000_000, bytes_accessed=10_000_000, transcendentals=0
            ),
            name="global_part",
        )(pos, *ins)

    near = []
    for c, piece in enumerate(pieces):
        slots = {0: piece}
        for i in range(bits):
            bit = 1 << ((i + c) % bits)
            slots[bit] = swap(piece, bit * pair)
        near.append(slots)

    locals_ = [run_local(0)]
    mark = locals_[0][-1]
    flat = [s[1 << i] for s in near for i in range(bits)]
    flat = tie(*flat, mark)[:-1]
    gathered = []
    for c in range(pair):
        got = {1 << i: flat[c * bits + i] for i in range(bits)}
        slots = {0: pieces[c]}
        for i in range(bits):
            bit = 1 << ((i + c) % bits)
            new = {}
            for o in sorted(slots):
                new[o | bit] = got[bit] if o == 0 else swap(slots[o], bit * pair)
            slots.update(new)
        gathered.append(slots)
    power = squares
    for x in tie(*others, mark)[:-1]:
        power = power + x
    inv_power = 1.0 / (power / (head_count * head_axis * width) + 1e-05)
    if pair > 1:
        inv_got = swap(inv_power, 1)
    for i in range(1, count):
        locals_.append(run_local(i))
    mark = locals_[-1][-1]
    if pair > 1:
        inv_got = tie(inv_got, mark)[0]
        inv_power = cat(
            [jnp.where(first, inv_power, inv_got), jnp.where(first, inv_got, inv_power)], 1
        )
    flat = [g[o] for o in range(units) for g in gathered]
    kv_all = cat(tie(*flat, mark)[:-1], 0).reshape(units, tokens, 2 * width)

    share = width // units
    grads, arrived = [], []
    for i in range(count):
        grad = run_global(i, locals_[i], kv_all, inv_power)
        grads.append(grad[:, :share])
        arrived.append(
            [swap(grad[:, o * share : (o + 1) * share], o * pair) for o in range(1, units)]
        )
        mark = grad
    totals = []
    for i in range(count):
        total = grads[i]
        parts = arrived[i]
        if i < count - 1:
            parts = tie(*parts, mark)[:-1]
        for x in parts:
            total = total + x
        totals.append(total)
    total = cat(totals, 0)
    if pair > 1:
        rows = share // pair
        keep = total[:, :rows]
        got = swap(total[:, rows:], 1)
        total = cat([jnp.where(first, keep, got), jnp.where(first, got, keep)], 0)
    return total[..., :half], total[..., half:]


def solution(mesh):
    return jax.shard_map(
        functools.partial(on_device, (mesh.shape["seq"], mesh.shape["head"])),
        mesh=mesh,
        in_specs=(
            P("seq", "head"),
            P("seq", "head"),
            P("seq", "head"),
            P("seq", "head"),
            P("head", None, None),
            P("head", None, None),
        ),
        out_specs=(P("head", "seq", None), P("head", "seq", None)),
        check_vma=False,
    )
```

time: 343 us -> 141 us (0.41); the launches traced: 337 us -> 140 us
  matrix products: 147 us -> 0 us
  waiting for transfers between devices: 108 us -> 10.6 us
  Pallas kernels: 0 us -> 71.3 us
  starting transfers between devices: 0.16 us -> 42.1 us
  blocking collectives: 33.8 us -> 0 us
  local copies, waits for them, and re-layouts: 26.5 us -> 5.69 us
  between operations: 14.4 us -> 0.9 us
    dot_general x20 -> x0, matrix products: 147 us -> none  [the longest x1 22.8 us: on_device(): jnp.einsum('r,rhfd->hfd', upper_mask, pieces[0], precision=exact_mode)]
    pallas_call x0 -> x4, Pallas kernels: none -> 71.3 us  [the longest x2 49.7 us: run_global(): pl.pallas_call(functools.partial(global_kernel, pair, units, block, width...]
    reduce_scatter x2 -> x0, waiting for transfers between devices: 55.2 us -> none  [the longest x1 42.5 us: on_device(): lax.psum_scatter(local_gk, 'seq', scatter_dimension=1, tiled=True)]
    all_gather x2 -> x0, waiting for transfers between devices: 52.5 us -> none  [the longest x1 26.4 us: on_device(): lax.all_gather(local_gstate[None], 'seq', axis=0, tiled=True)]
    ppermute x0 -> x22, starting transfers between devices: none -> 42.1 us  [the longest x19 33.5 us: swap(): return lax.ppermute(x, 'seq', [(i, i ^ bit) for i in range(seq_count)])]
    all_gather x2 -> x0, blocking collectives: 20 us -> none  [the longest x1 10.2 us: on_device(): lax.all_gather(local_total[None], 'seq', axis=0, tiled=True)]
    psum x1 -> x0, blocking collectives: 13.8 us -> none  [on_device(): power = lax.psum(local_power, 'head') / (HEADS * DH) + 1e-05]
    unnamed x57 -> x15, local copies, waits for them, and re-layouts: 12.4 us -> 1.49 us
  transfers between devices with their start and end apart: 4 -> 22, of which waited for: 4 -> 6; matrix products, arithmetic and copies ran while one was open for 38% -> 6% of each run, Pallas kernels for 0% -> 51%
where the time goes in v1:
time: 141 us; the launch traced here: 140 us
  Pallas kernels  71.3 us (51%)
  starting transfers between devices  42.1 us (30%)
  waiting for transfers between devices  10.6 us (8%)
  other arithmetic  9.74 us (7%)
  local copies, waits for them, and re-layouts  5.69 us (4%)
    pallas_call x2, Pallas kernels, run_global(): pl.pallas_call(functools.partial(global_kernel, pair, units, block, width...  49.7 us
    ppermute x19, starting transfers between devices, swap(): return lax.ppermute(x, 'seq', [(i, i ^ bit) for i in range(seq_count)])  33.5 us
    pallas_call x2, Pallas kernels, run_local(): pl.pallas_call(functools.partial(local_kernel, pair, block, width, half),...  21.5 us
    ppermute x19, waiting for transfers between devices, swap(): return lax.ppermute(x, 'seq', [(i, i ^ bit) for i in range(seq_count)])  10.6 us
    ppermute x3, starting transfers between devices, on_device(): lax.ppermute(squares, 'head', [(i, (i + s) % head_axis) for i in range(he...  8.55 us
    convert_element_type x2, other arithmetic, away(): lax.dynamic_slice_in_dim(source, start, sizes[i] * width, 1).astype(F32)  4.38 us
  transfers between devices with their start and end apart: 22, of which 6 were waited for; matrix products, arithmetic and copies ran while one was open for 6% of the time, Pallas kernels for 51%

profile of v1, /device:TPU:0, one launch (start us, length us, event | category | flops | bytes accessed | tf_op | source)
XLA Modules:
  0.0 140.2 jit_solution(2114689950113905204)
XLA Ops:
  0.7 1.1 constant_dynamic-slice_fusion
  1.8 2.8 %dynamic-slice_convert_fusion.3 = (f32[256,1024]{1,0:T(8,128)}, f32[256,1024]{1,0:T(8,128)}) fusion(bf16[256,4096]{1,0:T(8,128)(2,1)} %refs_0_.3, s32[]{:T(128)S(6)} %select_n.67, s32[]{:T(128)S(6)} %select_n.72), kind=kLoop, calls=%fused_computation.5 | loop fusion | flops 524288 | bytes 3145736 | tf_op jit(solution)/shard_map/convert_element_type | solution.py:293
  6.1 1.9 %collective-permute-done.1 = f32[256,256]{1,0:T(8,128)S(1)} collective-permute-done((f32[256,256]{1,0:T(8,128)S(1)}, f32[256,256]{1,0:T(8,128)S(1)}, u32[]{:S(2)}, u32[]{:S(2)}) %collective-permute-start.1) | collective-permute-done | bytes 262176 | tf_op jit(solution)/shard_map/ppermute | solution.py:271
  8.0 2.9 %collective-permute-start.10 = (f32[256,256]{1,0:T(8,128)S(1)}, f32[256,256]{1,0:T(8,128)S(1)}, u32[]{:S(2)}, u32[]{:S(2)}) collective-permute-start(f32[256,256]{1,0:T(8,128)S(1)} %get-tuple-element.58), channel_id=1, source_target_pairs={{0,8},{4,12},{8,0},{12,4},{16,24},{20,28},{24,16},{28,20},{1,9},{5... | collective-permute-start | bytes 786440 | tf_op jit(solution)/shard_map/ppermute | solution.py:271
  10.9 1.5 %collective-permute-start.11 = (f32[256,256]{1,0:T(8,128)S(1)}, f32[256,256]{1,0:T(8,128)S(1)}, u32[]{:S(2)}, u32[]{:S(2)}) collective-permute-start(f32[256,256]{1,0:T(8,128)S(1)} %get-tuple-element.58), channel_id=1, source_target_pairs={{0,16},{4,20},{8,24},{12,28},{16,0},{20,4},{24,8},{28,12},{1,17},{... | collective-permute-start | bytes 786440 | tf_op jit(solution)/shard_map/ppermute | solution.py:271
  13.0 1.6 %dynamic-slice_convert_fusion.1 = (f32[256,1024]{1,0:T(8,128)}, f32[256,1024]{1,0:T(8,128)}) fusion(bf16[256,4096]{1,0:T(8,128)(2,1)S(1)} %copy-done, s32[]{:T(128)S(6)} %select_n.67, s32[]{:T(128)S(6)} %select_n.72), kind=kLoop, calls=%fused_computation.3 | loop fusion | flops 524288 | bytes 3145736 | tf_op jit(solution)/shard_map/convert_element_type | solution.py:293
  15.1 0.9 pad_maximum_fusion.refs_4_
  16.0 2.1 %collective-permute-done.10 = f32[256,256]{1,0:T(8,128)S(1)} collective-permute-done((f32[256,256]{1,0:T(8,128)S(1)}, f32[256,256]{1,0:T(8,128)S(1)}, u32[]{:S(2)}, u32[]{:S(2)}) %collective-permute-start.10) | collective-permute-done | bytes 262176 | tf_op jit(solution)/shard_map/ppermute | solution.py:271
  18.1 2.1 %collective-permute-start.3 = (f32[1,256]{1,0:T(1,128)S(1)}, f32[1,256]{1,0:T(1,128)S(1)}, u32[]{:S(2)}, u32[]{:S(2)}) collective-permute-start(f32[1,256]{1,0:T(1,128)S(1)} %bitcast.8), channel_id=1, source_target_pairs={{0,1},{1,2},{2,3},{3,0},{4,5},{5,6},{6,7},{7,4},{8,9},{9,10},{10,1... | collective-permute-start | bytes 3080 | tf_op jit(solution)/shard_map/ppermute | solution.py:306
  20.2 2.6 %collective-permute-start.4 = (f32[1,256]{1,0:T(1,128)S(1)}, f32[1,256]{1,0:T(1,128)S(1)}, u32[]{:S(2)}, u32[]{:S(2)}) collective-permute-start(f32[1,256]{1,0:T(1,128)S(1)} %bitcast.9), channel_id=1, source_target_pairs={{0,2},{1,3},{2,0},{3,1},{4,6},{5,7},{6,4},{7,5},{8,10},{9,11},{10,... | collective-permute-start | bytes 3080 | tf_op jit(solution)/shard_map/ppermute | solution.py:306
  23.2 3.9 %collective-permute-start.5 = (f32[1,256]{1,0:T(1,128)S(1)}, f32[1,256]{1,0:T(1,128)S(1)}, u32[]{:S(2)}, u32[]{:S(2)}) collective-permute-start(f32[1,256]{1,0:T(1,128)S(1)} %bitcast.10), channel_id=1, source_target_pairs={{0,3},{1,0},{2,1},{3,2},{4,7},{5,4},{6,5},{7,6},{8,11},{9,8},{10,9... | collective-permute-start | bytes 3080 | tf_op jit(solution)/shard_map/ppermute | solution.py:306
  27.0 1.5 %collective-permute-start.9 = (f32[256,256]{1,0:T(8,128)S(1)}, f32[256,256]{1,0:T(8,128)S(1)}, u32[]{:S(2)}, u32[]{:S(2)}) collective-permute-start(f32[256,256]{1,0:T(8,128)S(1)} %get-tuple-element.57), channel_id=1, source_target_pairs={{0,16},{4,20},{8,24},{12,28},{16,0},{20,4},{24,8},{28,12},{1,17},{... | collective-permute-start | bytes 786440 | tf_op jit(solution)/shard_map/ppermute | solution.py:271
  28.5 10.8 %local_part.2 = (bf16[8,512,128]{2,1,0:T(8,128)(2,1)}, bf16[8,128,512]{2,1,0:T(8,128)(2,1)}, bf16[8,128,512]{2,1,0:T(8,128)(2,1)}, bf16[8,128,512]{2,1,0:T(8,128...) custom-call(s32[2]{0:T(128)} %pad_add_fusion.pos_ref, ...), custom_call_target="tpu_custom_call" | custom-call | flops 6144000000 | bytes 10000000 | tf_op jit(solution)/shard_map/local_part/pallas_call | solution.py:338
  40.5 1.5 %collective-permute-start.13 = (f32[256,256]{1,0:T(8,128)S(1)}, f32[256,256]{1,0:T(8,128)}, u32[]{:S(2)}, u32[]{:S(2)}) collective-permute-start(f32[256,256]{1,0:T(8,128)S(1)} %collective-permute-done.11), channel_id=1, source_target_pairs={{0,8},{4,12},{8,0},{12,4},{16,24},{20,28},{24,16},{28,20},{1,9},{5... | collective-permute-start | bytes 786440 | tf_op jit(solution)/shard_map/ppermute | solution.py:271
  42.1 10.7 %local_part.3 = (bf16[8,512,128]{2,1,0:T(8,128)(2,1)}, bf16[8,128,512]{2,1,0:T(8,128)(2,1)}, bf16[8,128,512]{2,1,0:T(8,128)(2,1)}, bf16[8,128,512]{2,1,0:T(8,128...) custom-call(s32[2]{0:T(128)} %pad_add_fusion.pos_ref, ...), custom_call_target="tpu_custom_call" | custom-call | flops 6144000000 | bytes 10000000 | tf_op jit(solution)/shard_map/local_part/pallas_call | solution.py:338
  52.8 0.6 pad_maximum_fusion.4.refs_10_
  53.5 1.0 constant_dynamic-update-slice_fusion
  54.5 1.3 copy-done.3
  55.9 24.9 %global_part.2 = f32[8,128,128]{2,1,0:T(8,128)} custom-call(s32[2]{0:T(128)} %pad_add_fusion.pos_ref, bf16[8,512,128]{2,1,0:T(8,128)(2,1)} %get-tuple-element.40.refs_0_, bf16[8,128,512]{2,1,0:T(8,128)(2,1)} %get-tuple-element.41.refs_1_, bf16[8,128,512]{2,1,0:T(8,128)(2,1)} %get-tuple-element.42.refs_2_, bf16[8,128,512]{2,1,0:T(8,128)(2,1)} %get-tuple-element.43.refs_3_, ...), custom_call_target="tpu_custom_call" | custom-call | flops 12288000000 | bytes 10000000 | tf_op jit(solution)/shard_map/global_part/pallas_call | solution.py:381
  80.8 1.1 fusion.5
  81.8 3.5 %collective-permute-start.14 = (f32[8,32,128]{2,1,0:T(8,128)S(1)}, f32[8,32,128]{2,1,0:T(8,128)S(1)}, u32[]{:S(2)}, u32[]{:S(2)}) collective-permute-start(f32[8,32,128]{2,1,0:T(8,128)S(1)} %get-tuple-element.80), channel_id=1, source_target_pairs={{0,8},{4,12},{8,0},{12,4},{16,24},{20,28},{24,16},{28,20},{1,9},{5... | collective-permute-start | bytes 393224 | tf_op jit(solution)/shard_map/ppermute | solution.py:271
  85.4 7.4 %collective-permute-start.15 = (f32[8,32,128]{2,1,0:T(8,128)S(1)}, f32[8,32,128]{2,1,0:T(8,128)S(1)}, u32[]{:S(2)}, u32[]{:S(2)}) collective-permute-start(f32[8,32,128]{2,1,0:T(8,128)S(1)} %get-tuple-element.79), channel_id=1, source_target_pairs={{0,16},{4,20},{8,24},{12,28},{16,0},{20,4},{24,8},{28,12},{1,17},{... | collective-permute-start | bytes 393224 | tf_op jit(solution)/shard_map/ppermute | solution.py:271
  92.8 24.9 %global_part.3 = f32[8,128,128]{2,1,0:T(8,128)} custom-call(s32[2]{0:T(128)} %pad_add_fusion.pos_ref, bf16[8,512,128]{2,1,0:T(8,128)(2,1)} %get-tuple-element.65.refs_0_, bf16[8,128,512]{2,1,0:T(8,128)(2,1)} %get-tuple-element.66.refs_1_, bf16[8,128,512]{2,1,0:T(8,128)(2,1)} %get-tuple-element.67.refs_2_, bf16[8,128,512]{2,1,0:T(8,128)(2,1)} %get-tuple-element.68.refs_3_, ...), custom_call_target="tpu_custom_call" | custom-call | flops 12288000000 | bytes 10000000 | tf_op jit(solution)/shard_map/global_part/pallas_call | solution.py:381
  117.6 1.1 fusion.6
  118.7 4.5 %collective-permute-start.18 = (f32[8,32,128]{2,1,0:T(8,128)S(1)}, f32[8,32,128]{2,1,0:T(8,128)S(1)}, u32[]{:S(2)}, u32[]{:S(2)}) collective-permute-start(f32[8,32,128]{2,1,0:T(8,128)S(1)} %get-tuple-element.81), channel_id=1, source_target_pairs={{0,8},{4,12},{8,0},{12,4},{16,24},{20,28},{24,16},{28,20},{1,9},{5... | collective-permute-start | bytes 393224 | tf_op jit(solution)/shard_map/ppermute | solution.py:271
  123.2 7.9 %collective-permute-start.19 = (f32[8,32,128]{2,1,0:T(8,128)S(1)}, f32[8,32,128]{2,1,0:T(8,128)S(1)}, u32[]{:S(2)}, u32[]{:S(2)}) collective-permute-start(f32[8,32,128]{2,1,0:T(8,128)S(1)} %get-tuple-element.83), channel_id=1, source_target_pairs={{0,16},{4,20},{8,24},{12,28},{16,0},{20,4},{24,8},{28,12},{1,17},{... | collective-permute-start | bytes 393224 | tf_op jit(solution)/shard_map/ppermute | solution.py:271
  131.1 0.9 fusion.4
  132.1 4.1 %collective-permute-done.19 = f32[8,32,128]{2,1,0:T(8,128)S(1)} collective-permute-done((f32[8,32,128]{2,1,0:T(8,128)S(1)}, f32[8,32,128]{2,1,0:T(8,128)S(1)}, u32[]{:S(2)}, u32[]{:S(2)}) %collective-permute-start.19) | collective-permute-done | bytes 131104 | tf_op jit(solution)/shard_map/ppermute | solution.py:271
  136.2 0.8 collective-permute-done.20
  137.0 0.9 fusion.2
  138.0 1.3 collective-permute-done.21
  139.4 0.9 pad_maximum_fusion.1
  (50 shorter events, 4.5 us)
Async XLA Ops:
  0.6 5.0 %copy-start = (bf16[256,4096]{1,0:T(8,128)(2,1)S(1)}, bf16[256,4096]{1,0:T(8,128)(2,1)}, u32[]{:S(2)}) copy-start(bf16[256,4096]{1,0:T(8,128)(2,1)} %refs_8_.3) | copy-start | bytes 6291460
  4.6 22.4 %collective-permute-start = (f32[256,1024]{1,0:T(8,128)}, f32[256,1024]{1,0:T(8,128)}, u32[]{:S(2)}, u32[]{:S(2)}) collective-permute-start(f32[256,1024]{1,0:T(8,128)} %get-tuple-element.76), channel_id=1, source_target_pairs={{0,4},{4,0},{8,12},{12,8},{16,20},{20,16},{24,28},{28,24},{1,5},{5... | collective-permute-start | bytes 3145736 | tf_op jit(solution)/shard_map/ppermute | solution.py:271
  5.1 2.9 %collective-permute-start.1 = (f32[256,256]{1,0:T(8,128)S(1)}, f32[256,256]{1,0:T(8,128)S(1)}, u32[]{:S(2)}, u32[]{:S(2)}) collective-permute-start(f32[256,256]{1,0:T(8,128)S(1)} %maximum_convert_fusion), channel_id=1, source_target_pairs={{0,4},{4,0},{8,12},{12,8},{16,20},{20,16},{24,28},{28,24},{1,5},{5... | collective-permute-start | bytes 786440 | tf_op jit(solution)/shard_map/ppermute | solution.py:271
  5.1 36.8 %collective-permute-start.7 = (f32[256,1024]{1,0:T(8,128)}, f32[256,1024]{1,0:T(8,128)}, u32[]{:S(2)}, u32[]{:S(2)}) collective-permute-start(f32[256,1024]{1,0:T(8,128)} %get-tuple-element.77), channel_id=1, source_target_pairs={{0,4},{4,0},{8,12},{12,8},{16,20},{20,16},{24,28},{28,24},{1,5},{5... | collective-permute-start | bytes 3145736 | tf_op jit(solution)/shard_map/ppermute | solution.py:271
  8.0 10.1 %collective-permute-start.10 = (f32[256,256]{1,0:T(8,128)S(1)}, f32[256,256]{1,0:T(8,128)S(1)}, u32[]{:S(2)}, u32[]{:S(2)}) collective-permute-start(f32[256,256]{1,0:T(8,128)S(1)} %get-tuple-element.58), channel_id=1, source_target_pairs={{0,8},{4,12},{8,0},{12,4},{16,24},{20,28},{24,16},{28,20},{1,9},{5... | collective-permute-start | bytes 786440 | tf_op jit(solution)/shard_map/ppermute | solution.py:271
  10.9 9.3 %collective-permute-start.11 = (f32[256,256]{1,0:T(8,128)S(1)}, f32[256,256]{1,0:T(8,128)S(1)}, u32[]{:S(2)}, u32[]{:S(2)}) collective-permute-start(f32[256,256]{1,0:T(8,128)S(1)} %get-tuple-element.58), channel_id=1, source_target_pairs={{0,16},{4,20},{8,24},{12,28},{16,0},{20,4},{24,8},{28,12},{1,17},{... | collective-permute-start | bytes 786440 | tf_op jit(solution)/shard_map/ppermute | solution.py:271
  12.5 10.7 %collective-permute-start.8 = (f32[256,256]{1,0:T(8,128)S(1)}, f32[256,256]{1,0:T(8,128)S(1)}, u32[]{:S(2)}, u32[]{:S(2)}) collective-permute-start(f32[256,256]{1,0:T(8,128)S(1)} %get-tuple-element.57), channel_id=1, source_target_pairs={{0,8},{4,12},{8,0},{12,4},{16,24},{20,28},{24,16},{28,20},{1,9},{5... | collective-permute-start | bytes 786440 | tf_op jit(solution)/shard_map/ppermute | solution.py:271
  18.1 21.4 %collective-permute-start.3 = (f32[1,256]{1,0:T(1,128)S(1)}, f32[1,256]{1,0:T(1,128)S(1)}, u32[]{:S(2)}, u32[]{:S(2)}) collective-permute-start(f32[1,256]{1,0:T(1,128)S(1)} %bitcast.8), channel_id=1, source_target_pairs={{0,1},{1,2},{2,3},{3,0},{4,5},{5,6},{6,7},{7,4},{8,9},{9,10},{10,1... | collective-permute-start | bytes 3080 | tf_op jit(solution)/shard_map/ppermute | solution.py:306
  20.2 19.7 %collective-permute-start.4 = (f32[1,256]{1,0:T(1,128)S(1)}, f32[1,256]{1,0:T(1,128)S(1)}, u32[]{:S(2)}, u32[]{:S(2)}) collective-permute-start(f32[1,256]{1,0:T(1,128)S(1)} %bitcast.9), channel_id=1, source_target_pairs={{0,2},{1,3},{2,0},{3,1},{4,6},{5,7},{6,4},{7,5},{8,10},{9,11},{10,... | collective-permute-start | bytes 3080 | tf_op jit(solution)/shard_map/ppermute | solution.py:306
  23.2 17.3 %collective-permute-start.5 = (f32[1,256]{1,0:T(1,128)S(1)}, f32[1,256]{1,0:T(1,128)S(1)}, u32[]{:S(2)}, u32[]{:S(2)}) collective-permute-start(f32[1,256]{1,0:T(1,128)S(1)} %bitcast.10), channel_id=1, source_target_pairs={{0,3},{1,0},{2,1},{3,2},{4,7},{5,4},{6,5},{7,6},{8,11},{9,8},{10,9... | collective-permute-start | bytes 3080 | tf_op jit(solution)/shard_map/ppermute | solution.py:306
  27.0 12.3 %collective-permute-start.9 = (f32[256,256]{1,0:T(8,128)S(1)}, f32[256,256]{1,0:T(8,128)S(1)}, u32[]{:S(2)}, u32[]{:S(2)}) collective-permute-start(f32[256,256]{1,0:T(8,128)S(1)} %get-tuple-element.57), channel_id=1, source_target_pairs={{0,16},{4,20},{8,24},{12,28},{16,0},{20,4},{24,8},{28,12},{1,17},{... | collective-permute-start | bytes 786440 | tf_op jit(solution)/shard_map/ppermute | solution.py:271
  28.5 10.8 %copy-start.2 = (f32[256,1024]{1,0:T(8,128)S(1)}, f32[256,1024]{1,0:T(8,128)}, u32[]{:S(2)}) copy-start(f32[256,1024]{1,0:T(8,128)} %get-tuple-element.74) | copy-start | bytes 3145732
  28.5 10.9 %copy-start.1 = (f32[256,1024]{1,0:T(8,128)S(1)}, f32[256,1024]{1,0:T(8,128)}, u32[]{:S(2)}) copy-start(f32[256,1024]{1,0:T(8,128)} %get-tuple-element.75) | copy-start | bytes 3145732
  39.4 15.2 %collective-permute-start.2 = (f32[256,1024]{1,0:T(8,128)S(1)}, f32[256,1024]{1,0:T(8,128)}, u32[]{:S(2)}, u32[]{:S(2)}) collective-permute-start(f32[256,1024]{1,0:T(8,128)S(1)} %copy-done.2), channel_id=1, source_target_pairs={{0,4},{4,0},{8,12},{12,8},{16,20},{20,16},{24,28},{28,24},{1,5},{5... | collective-permute-start | bytes 3145736 | tf_op jit(solution)/shard_map/ppermute | solution.py:271
  39.5 53.3 %collective-permute-start.17 = (f32[256,1024]{1,0:T(8,128)S(1)}, f32[256,1024]{1,0:T(8,128)}, u32[]{:S(2)}, u32[]{:S(2)}) collective-permute-start(f32[256,1024]{1,0:T(8,128)S(1)} %copy-done.1), channel_id=1, source_target_pairs={{0,4},{4,0},{8,12},{12,8},{16,20},{20,16},{24,28},{28,24},{1,5},{5... | collective-permute-start | bytes 3145736 | tf_op jit(solution)/shard_map/ppermute | solution.py:271
  40.0 13.4 %collective-permute-start.12 = (f32[256,256]{1,0:T(8,128)S(1)}, f32[256,256]{1,0:T(8,128)S(1)}, u32[]{:S(2)}, u32[]{:S(2)}) collective-permute-start(f32[256,256]{1,0:T(8,128)S(1)} %collective-permute-done.8), channel_id=1, source_target_pairs={{0,16},{4,20},{8,24},{12,28},{16,0},{20,4},{24,8},{28,12},{1,17},{... | collective-permute-start | bytes 786440 | tf_op jit(solution)/shard_map/ppermute | solution.py:271
  40.5 12.9 %collective-permute-start.13 = (f32[256,256]{1,0:T(8,128)S(1)}, f32[256,256]{1,0:T(8,128)}, u32[]{:S(2)}, u32[]{:S(2)}) collective-permute-start(f32[256,256]{1,0:T(8,128)S(1)} %collective-permute-done.11), channel_id=1, source_target_pairs={{0,8},{4,12},{8,0},{12,4},{16,24},{20,28},{24,16},{28,20},{1,9},{5... | collective-permute-start | bytes 786440 | tf_op jit(solution)/shard_map/ppermute | solution.py:271
  42.0 10.8 %collective-permute-start.6 = (f32[1,256]{1,0:T(1,128)S(1)}, f32[1,256]{1,0:T(1,128)S(1)}, u32[]{:S(2)}, u32[]{:S(2)}) collective-permute-start(f32[1,256]{1,0:T(1,128)S(1)} %add_divide_fusion), channel_id=1, source_target_pairs={{0,4},{4,0},{8,12},{12,8},{16,20},{20,16},{24,28},{28,24},{1,5},{5... | collective-permute-start | bytes 3080 | tf_op jit(solution)/shard_map/ppermute | solution.py:271
  54.5 1.4 copy-start.3
  81.8 49.3 %collective-permute-start.14 = (f32[8,32,128]{2,1,0:T(8,128)S(1)}, f32[8,32,128]{2,1,0:T(8,128)S(1)}, u32[]{:S(2)}, u32[]{:S(2)}) collective-permute-start(f32[8,32,128]{2,1,0:T(8,128)S(1)} %get-tuple-element.80), channel_id=1, source_target_pairs={{0,8},{4,12},{8,0},{12,4},{16,24},{20,28},{24,16},{28,20},{1,9},{5... | collective-permute-start | bytes 393224 | tf_op jit(solution)/shard_map/ppermute | solution.py:271
  85.4 45.7 %collective-permute-start.15 = (f32[8,32,128]{2,1,0:T(8,128)S(1)}, f32[8,32,128]{2,1,0:T(8,128)S(1)}, u32[]{:S(2)}, u32[]{:S(2)}) collective-permute-start(f32[8,32,128]{2,1,0:T(8,128)S(1)} %get-tuple-element.79), channel_id=1, source_target_pairs={{0,16},{4,20},{8,24},{12,28},{16,0},{20,4},{24,8},{28,12},{1,17},{... | collective-permute-start | bytes 393224 | tf_op jit(solution)/shard_map/ppermute | solution.py:271
  92.8 38.3 %collective-permute-start.16 = (f32[8,32,128]{2,1,0:T(8,128)S(1)}, f32[8,32,128]{2,1,0:T(8,128)S(1)}, u32[]{:S(2)}, u32[]{:S(2)}) collective-permute-start(f32[8,32,128]{2,1,0:T(8,128)S(1)} %get-tuple-element.78), channel_id=1, source_target_pairs={{0,24},{4,28},{8,16},{12,20},{16,8},{20,12},{24,0},{28,4},{1,25},{... | collective-permute-start | bytes 393224 | tf_op jit(solution)/shard_map/ppermute | solution.py:271
  118.7 13.4 %collective-permute-start.18 = (f32[8,32,128]{2,1,0:T(8,128)S(1)}, f32[8,32,128]{2,1,0:T(8,128)S(1)}, u32[]{:S(2)}, u32[]{:S(2)}) collective-permute-start(f32[8,32,128]{2,1,0:T(8,128)S(1)} %get-tuple-element.81), channel_id=1, source_target_pairs={{0,8},{4,12},{8,0},{12,4},{16,24},{20,28},{24,16},{28,20},{1,9},{5... | collective-permute-start | bytes 393224 | tf_op jit(solution)/shard_map/ppermute | solution.py:271
  123.2 13.0 %collective-permute-start.19 = (f32[8,32,128]{2,1,0:T(8,128)S(1)}, f32[8,32,128]{2,1,0:T(8,128)S(1)}, u32[]{:S(2)}, u32[]{:S(2)}) collective-permute-start(f32[8,32,128]{2,1,0:T(8,128)S(1)} %get-tuple-element.83), channel_id=1, source_target_pairs={{0,16},{4,20},{8,24},{12,28},{16,0},{20,4},{24,8},{28,12},{1,17},{... | collective-permute-start | bytes 393224 | tf_op jit(solution)/shard_map/ppermute | solution.py:271
  131.1 5.9 %collective-permute-start.20 = (f32[8,32,128]{2,1,0:T(8,128)S(1)}, f32[8,32,128]{2,1,0:T(8,128)S(1)}, u32[]{:S(2)}, u32[]{:S(2)}) collective-permute-start(f32[8,32,128]{2,1,0:T(8,128)S(1)} %get-tuple-element.82), channel_id=1, source_target_pairs={{0,24},{4,28},{8,16},{12,20},{16,8},{20,12},{24,0},{28,4},{1,25},{... | collective-permute-start | bytes 393224 | tf_op jit(solution)/shard_map/ppermute | solution.py:271
  137.9 1.4 %collective-permute-start.21 = (f32[16,16,128]{2,1,0:T(8,128)S(1)}, f32[16,16,128]{2,1,0:T(8,128)S(1)}, u32[]{:S(2)}, u32[]{:S(2)}) collective-permute-start(f32[16,16,128]{2,1,0:T(8,128)S(1)} %pad_maximum_fusion.2), channel_id=1, source_target_pairs={{0,4},{4,0},{8,12},{12,8},{16,20},{20,16},{24,28},{28,24},{1,5},{5... | collective-permute-start | bytes 393224 | tf_op jit(solution)/shard_map/ppermute | solution.py:271

commit v2 on v1

--- a/solution.py
+++ b/solution.py
@@ -10,8 +10,8 @@
 F32, BF16 = jnp.float32, jnp.bfloat16
 LANES = 128
 ROWS = 16
-STEP_A = 2
-STEP_B = 4
+STEP_A = 4
+STEP_B = 8
 PARTS = (1, 1)
 VMEM_LIMIT = 60 * 1024 * 1024
 
@@ -78,8 +78,10 @@
         v_tr[width:] = jnp.ones((ROWS, tokens), BF16)
 
     mask = causal_mask(block)
-    k_logits = mm_nt(wk[...].reshape(heads * half, width), k_nat[...])
-    for h in range(heads):
+    each = range(heads)
+    spans = [slice(b * block, (b + 1) * block) for b in range(pair)]
+    chains = [(h, b) for h in each for b in range(pair)]
+    for h in each:
         cols = slice(h * width, (h + 1) * width)
         if pair > 1:
             place = pos_ref[0]
@@ -89,24 +91,29 @@
             ].astype(BF16)
         else:
             q_out[h] = q_own[:, cols]
-        qh, ql = split(features(mm_nt(wq[h], q_out[h])))
-        kh, kl = split(features(k_logits[h * half : (h + 1) * half]))
-        qh_out[h] = qh
-        ql_out[h] = ql
-        kh_out[h] = kh
-        kl_out[h] = kl
-        for b in range(pair):
-            at = slice(b * block, (b + 1) * block)
-            kth, ktl = kh[:, at].T, kl[:, at].T
-            scores = mm(cat([kth, kth, ktl], 1), cat([qh[:, at], ql[:, at], qh[:, at]], 0))
-            sh, sl = split(jnp.where(mask, scores, 0.0))
-            vt = v_tr[:, at]
-            num_out[h, b] = mm(cat([vt, vt], 1), cat([sh, sl], 0))
-        if pair > 1:
-            va = v_aug[:block]
+    k_logits = mm_nt(wk[...].reshape(heads * half, width), k_nat[...])
+    q_logits = [mm_nt(wq[h], q_out[h]) for h in each]
+    k_parts = [split(features(k_logits[h * half : (h + 1) * half])) for h in each]
+    q_parts = [split(features(q_logits[h])) for h in each]
+    for h in each:
+        kh_out[h], kl_out[h] = k_parts[h]
+        qh_out[h], ql_out[h] = q_parts[h]
+    turned = [(k_parts[h][0][:, spans[b]].T, k_parts[h][1][:, spans[b]].T) for h, b in chains]
+    scores = []
+    for (h, b), (kth, ktl) in zip(chains, turned):
+        qh, ql = q_parts[h][0][:, spans[b]], q_parts[h][1][:, spans[b]]
+        scores.append(mm(cat([kth, kth, ktl], 1), cat([qh, ql, qh], 0)))
+    if pair > 1:
+        va = v_aug[:block]
+        for h in each:
+            kh, kl = k_parts[h]
             state_out[h] = mm(cat([kh[:, :block], kl[:, :block]], 1), cat([va, va], 0))
-        else:
-            state_out[h] = jnp.zeros(state_out.shape[1:], F32)
+    else:
+        state_out[...] = jnp.zeros_like(state_out)
+    masked = [split(jnp.where(mask, x, 0.0)) for x in scores]
+    for (h, b), (sh, sl) in zip(chains, masked):
+        vt = v_tr[:, spans[b]]
+        num_out[h, b] = mm(cat([vt, vt], 1), cat([sh, sl], 0))
 
 
 def global_kernel(pair, units, block, width, half, pos_ref, *refs):
@@ -114,9 +121,11 @@
     q, qh_in, ql_in, kh_in, kl_in, num_in, state_in, wk, t_own = refs[:9]
     refs = refs[9:]
     t_got = refs.pop(0) if pair > 1 else None
-    inv_power, kv = refs[:2]
-    out = refs[2]
-    k_nat, v_aug, v_tr, feat_old, state, grad_high, grad_low, grad_k, gsum = refs[3:]
+    inv_power = refs.pop(0)
+    kv, refs = refs[: units * pair], refs[units * pair :]
+    outs, refs = refs[:units], refs[units:]
+    k_nat, v_aug, feat_old, state, grad_k, gsum, turn = refs
+    two = 2 * half
     heads = wk.shape[0]
     tokens = pair * block
     place, unit = pos_ref[0], pos_ref[1]
@@ -124,13 +133,10 @@
     @pl.when(pl.program_id(0) == 0)
     def _():
         for o in range(units):
-            k_nat[o] = kv[o, :, :width].astype(BF16)
-            v = kv[o, :, width:]
-            v_aug[o] = with_ones(v).astype(BF16)
-            v_tr[o, :width] = v.T.astype(BF16)
-            v_tr[o, width:] = jnp.ones((width, tokens), BF16)
-        grad_high[...] = jnp.zeros_like(grad_high)
-        grad_low[...] = jnp.zeros_like(grad_low)
+            for c in range(pair):
+                at = slice(c * block, (c + 1) * block)
+                k_nat[o, at] = kv[o * pair + c][:, :width].astype(BF16)
+                v_aug[o, at] = with_ones(kv[o * pair + c][:, width:]).astype(BF16)
 
     wk_all = wk[...].reshape(heads * half, width)
     state[...] = jnp.zeros_like(state)
@@ -139,8 +145,8 @@
         o = unit ^ u
         logits = mm_nt(wk_all, k_nat[o])
         highs, lows = [], []
-        for h in range(heads):
-            feat = features(logits[h * half : (h + 1) * half])
+        feats = [features(logits[h * half : (h + 1) * half]) for h in range(heads)]
+        for h, feat in enumerate(feats):
             feat_old[u, h] = feat
             fh, fl = split(feat)
             highs.append(fh)
@@ -152,80 +158,96 @@
     lax.fori_loop(0, unit, ahead, 0)
 
     mask = causal_mask(block)
-    for h in range(heads):
-        total_state = state[h * 2 * half : (h + 1) * 2 * half]
-        grad_q = jnp.zeros((half, width), F32)
-        sums = []
-        key_grads = []
-        for b in range(pair):
-            at = slice(b * block, (b + 1) * block)
-            if b == 1:
-                total_state = total_state + state_in[h]
-            sth, stl = split(total_state)
-            turned = total_state.T[: width + ROWS]
-            tth, ttl = split(turned)
-            qh, ql = qh_in[h, :, at], ql_in[h, :, at]
-            kh, kl = kh_in[h, :, at], kl_in[h, :, at]
-            numer = num_in[h, b] + mm(cat([tth, tth, ttl], 1), cat([qh, ql, qh], 0))
-            inv = 1.0 / numer[width : width + 1]
-            student = numer[:width] * inv
-            own_t = t_own[:, h * width : (h + 1) * width].astype(F32)
-            if pair > 1:
-                own_t = jnp.where(place == b, own_t, t_got[:, h * width : (h + 1) * width])
-            grad_out = (student - own_t.T) * inv_power[0:1, at]
-            gnum = grad_out * inv
-            gden = -jnp.sum(grad_out * student, 0, keepdims=True) * inv
-            top = lax.broadcasted_iota(jnp.int32, (ROWS, block), 0) == 0
-            gh, gl = split(gnum)
-            dh, dl = split(jnp.where(top, gden, 0.0))
-            grad_high[:width] = gh
-            grad_low[:width] = gl
-            grad_high[width : width + ROWS] = dh
-            grad_low[width : width + ROWS] = dl
-            gah, gal = grad_high[...], grad_low[...]
-            va = v_aug[0, at]
-            back = mm(cat([va, va], 1), cat([gah, gal], 0))
-            bh, bl = split(jnp.where(mask, back, 0.0))
-            gq = mm(cat([sth, sth, stl], 1), cat([gah, gal, gah], 0)) + mm(
-                cat([kh, kh, kl], 1), cat([bh, bl, bh], 0)
-            )
-            q_feat = qh.astype(F32) + ql.astype(F32)
-            lh, ll = split(features_back(q_feat, gq))
-            q_nat = q[h, at]
-            grad_q = grad_q + mm(cat([lh, ll], 1), cat([q_nat, q_nat], 0))
-            small_h, small_l = gah[: width + ROWS], gal[: width + ROWS]
-            sums.append(
-                mm_nt(cat([small_h, small_h, small_l], 1), cat([qh, ql, qh], 1))
-            )
-            key_grads.append(mm_nt(cat([qh, qh, ql], 1), cat([bh, bl, bh], 1)))
-        grad_kk = jnp.zeros((half, width), F32)
+    each = range(heads)
+    spans = [slice(b * block, (b + 1) * block) for b in range(pair)]
+    chains = [(h, b) for h in each for b in range(pair)]
+
+    def three(x, y, axis_x, axis_y):
+        return cat([x[0], x[0], x[1]], axis_x), cat([y[0], y[1], y[0]], axis_y)
+
+    def feat_of(high, low):
+        return high.astype(F32) + low.astype(F32)
+
+    totals = []
+    for h, b in chains:
+        x = state[h * two : (h + 1) * two]
+        totals.append(x + state_in[h] if b == 1 else x)
+    states = [split(x) for x in totals]
+    turned = [
+        split(cat([x[:, :width].T, x[:, width : width + LANES].T[:ROWS]], 0)) for x in totals
+    ]
+    qs = [(qh_in[h, :, spans[b]], ql_in[h, :, spans[b]]) for h, b in chains]
+    ks = [(kh_in[h, :, spans[b]], kl_in[h, :, spans[b]]) for h, b in chains]
+    numers = [
+        num_in[h, b] + mm(*three(t, q_, 1, 0)) for (h, b), t, q_ in zip(chains, turned, qs)
+    ]
+    targets = []
+    for h, b in chains:
+        own_t = t_own[:, h * width : (h + 1) * width].astype(F32)
+        if pair > 1:
+            own_t = jnp.where(place == b, own_t, t_got[:, h * width : (h + 1) * width])
+        targets.append(own_t.T)
+    top = lax.broadcasted_iota(jnp.int32, (ROWS, block), 0) == 0
+    small, full = [], []
+    for (h, b), numer, target in zip(chains, numers, targets):
+        inv = 1.0 / numer[width : width + 1]
+        student = numer[:width] * inv
+        grad_out = (student - target) * inv_power[0:1, spans[b]]
+        gden = -jnp.sum(grad_out * student, 0, keepdims=True) * inv
+        gh, gl = split(grad_out * inv)
+        dh, dl = split(jnp.where(top, gden, 0.0))
+        pad = jnp.zeros((width - ROWS, block), BF16)
+        small.append((cat([gh, dh], 0), cat([gl, dl], 0)))
+        full.append((cat([gh, dh, pad], 0), cat([gl, dl, pad], 0)))
+    backs = []
+    for (h, b), g in zip(chains, full):
+        va = v_aug[0, spans[b]]
+        backs.append(mm(cat([va, va], 1), cat([g[0], g[1]], 0)))
+    grad_q = [mm(*three(st, g, 1, 0)) for st, g in zip(states, full)]
+    sums = [mm_nt(*three(g, q_, 1, 1)) for g, q_ in zip(small, qs)]
+    backs = [split(jnp.where(mask, x, 0.0)) for x in backs]
+    grad_q = [g + mm(*three(k, x, 1, 0)) for g, k, x in zip(grad_q, ks, backs)]
+    key_grads = [mm_nt(*three(q_, x, 1, 1)) for q_, x in zip(qs, backs)]
+
+    def widen(x):
+        return cat([x, jnp.zeros((width - ROWS, width), F32)], 0).T
+
+    wide = [widen(x) for x in sums]
+    for h in each:
         later = None
         for b in reversed(range(pair)):
-            at = slice(b * block, (b + 1) * block)
-            gk = key_grads[b]
+            n = h * pair + b
             if later is not None:
-                padded = cat([later, jnp.zeros((width - ROWS, width), F32)], 0).T
-                ph, pl_ = split(padded)
-                vt = v_tr[0, :, at]
-                gk = gk + mm(cat([ph, pl_], 1), cat([vt, vt], 0))
-            kh, kl = kh_in[h, :, at], kl_in[h, :, at]
-            k_feat = kh.astype(F32) + kl.astype(F32)
-            lh, ll = split(features_back(k_feat, gk))
-            k_blk = k_nat[0, at]
-            grad_kk = grad_kk + mm(cat([lh, ll], 1), cat([k_blk, k_blk], 0))
-            later = sums[b] if later is None else later + sums[b]
-        padded = cat([later, jnp.zeros((width - ROWS, width), F32)], 0).T
-        gsum[h * 2 * half : (h + 1) * 2 * half] = padded
-        grad_k[h, :half] = grad_q
-        grad_k[h, half:] = grad_kk
+                ph, plow = split(later)
+                va = v_aug[0, spans[b]]
+                key_grads[n] = key_grads[n] + mm_nt(cat([ph, plow], 1), cat([va, va], 1))
+            later = wide[n] if later is None else later + wide[n]
+        gsum[h * two : (h + 1) * two] = later
+    q_logit = [split(features_back(feat_of(*q_), g)) for q_, g in zip(qs, grad_q)]
+    k_logit = [split(features_back(feat_of(*k), g)) for k, g in zip(ks, key_grads)]
+    for h in each:
+        rows = range(h * pair, (h + 1) * pair)
+        left = cat([x for n in rows for x in q_logit[n]], 1)
+        right = cat([q[h, spans[b]] for b in range(pair) for _ in range(2)], 0)
+        grad_k[h, :half] = mm(left, right)
+    for b in range(pair):
+        highs = cat([k_logit[h * pair + b][0] for h in each], 0)
+        lows = cat([k_logit[h * pair + b][1] for h in each], 0)
+        k_blk = k_nat[0, spans[b]]
+        add = mm(cat([highs, lows], 1), cat([k_blk, k_blk], 0))
+        for h in each:
+            if b == 0:
+                grad_k[h, half:] = add[h * half : (h + 1) * half]
+            else:
+                grad_k[h, half:] += add[h * half : (h + 1) * half]
 
     gsh, gsl = split(gsum[...])
     both = cat([gsh, gsl], 1)
 
     def behind(u, carry):
         o = unit ^ u
-        vt = v_tr[o]
-        gk = mm(both, cat([vt, vt], 0))
+        va = v_aug[o]
+        gk = mm_nt(both, cat([va, va], 1))
         highs, lows = [], []
         for h in range(heads):
             lh, ll = split(
@@ -242,14 +264,13 @@
     lax.fori_loop(0, unit, behind, 0)
 
     share = width // (units * pair)
-    for h in range(heads):
-        flat = grad_k[h].T
-        for u in range(units):
+    for h in each:
+        turn[h] = grad_k[h].T
+    for h in each:
+        for o in range(units):
             for r in range(pair):
-                slot = (unit ^ u) * pair + (place ^ r)
-                start = pl.multiple_of(slot * share, share)
-                n = u * pair + r
-                out[h, pl.ds(start, share)] = flat[n * share : (n + 1) * share]
+                start = pl.multiple_of(((unit ^ o) * pair + (place ^ r)) * share, share)
+                outs[o][h, r * share : (r + 1) * share] = turn[h, pl.ds(start, share)]
 
 
 def on_device(axis_sizes, queries, keys, values, teacher, map_q, map_k):
@@ -359,7 +380,7 @@
         )(pos, *ins)
 
     def run_global(i, local, kv_all, inv_power):
-        n = min(STEP_B, sizes[i])
+        n = max(d for d in range(1, STEP_B + 1) if sizes[i] % d == 0 and begins[i] % d == 0)
         steps = sizes[i] // n
         index = lambda g, p: p[0] * (heads // n) + begins[i] // n + g
         ins = [*local, wk_t, teacher]
@@ -373,29 +394,25 @@
         if pair > 1:
             ins.append(t_got[i])
             in_specs.append(spec((block, n * width), lambda g, p: (0, g)))
-        ins += [inv_power, kv_all]
-        in_specs += [
-            spec((1, tokens), whole2),
-            spec((units, tokens, 2 * width), lambda g, p: (0, 0, 0)),
-        ]
+        ins += [inv_power, *kv_all]
+        in_specs.append(spec((1, tokens), whole2))
+        in_specs += [spec((block, 2 * width), whole2)] * len(kv_all)
         return pl.pallas_call(
             functools.partial(global_kernel, pair, units, block, width, half),
-            out_shape=jax.ShapeDtypeStruct((sizes[i], width, two), F32),
+            out_shape=[jax.ShapeDtypeStruct((sizes[i], width // units, two), F32)] * units,
             grid_spec=pltpu.PrefetchScalarGridSpec(
                 num_scalar_prefetch=1,
                 grid=(steps,),
                 in_specs=in_specs,
-                out_specs=spec((n, width, two), per_head3),
+                out_specs=[spec((n, width // units, two), per_head3)] * units,
                 scratch_shapes=[
                     pltpu.VMEM((units, tokens, width), BF16),
                     pltpu.VMEM((units, tokens, 2 * width), BF16),
-                    pltpu.VMEM((units, 2 * width, tokens), BF16),
                     pltpu.VMEM((max(units - 1, 1), n, two, tokens), F32),
                     pltpu.VMEM((n * two, 2 * width), F32),
-                    pltpu.VMEM((2 * width, block), BF16),
-                    pltpu.VMEM((2 * width, block), BF16),
                     pltpu.VMEM((n, two, width), F32),
                     pltpu.VMEM((n * two, 2 * width), F32),
+                    pltpu.VMEM((n, width, two), F32),
                 ],
             ),
             compiler_params=pltpu.CompilerParams(
@@ -445,22 +462,21 @@
             [jnp.where(first, inv_power, inv_got), jnp.where(first, inv_got, inv_power)], 1
         )
     flat = [g[o] for o in range(units) for g in gathered]
-    kv_all = cat(tie(*flat, mark)[:-1], 0).reshape(units, tokens, 2 * width)
+    kv_all = tie(*flat, mark)[:-1]
 
     share = width // units
-    grads, arrived = [], []
-    for i in range(count):
+    grads, arrived = [None] * count, [None] * count
+    order = sorted(range(count), key=lambda i: -sizes[i])
+    for i in order:
         grad = run_global(i, locals_[i], kv_all, inv_power)
-        grads.append(grad[:, :share])
-        arrived.append(
-            [swap(grad[:, o * share : (o + 1) * share], o * pair) for o in range(1, units)]
-        )
-        mark = grad
+        grads[i] = grad[0]
+        arrived[i] = [swap(grad[o], o * pair) for o in range(1, units)]
+        inv_power, mark = tie(inv_power, grad[0])
     totals = []
     for i in range(count):
         total = grads[i]
         parts = arrived[i]
-        if i < count - 1:
+        if i != order[-1]:
             parts = tie(*parts, mark)[:-1]
         for x in parts:
             total = total + x

time: 141 us -> 101 us (0.72)
  Pallas kernels: 71.3 us -> 44.5 us
  starting transfers between devices: 42.1 us -> 34.2 us
  local copies, waits for them, and re-layouts: 5.69 us -> 2.8 us
    pallas_call x2, Pallas kernels: 49.7 us -> 29.5 us  [run_global(): pl.pallas_call(functools.partial(global_kernel, pair, units, block, width...]
    pallas_call x2, Pallas kernels: 21.5 us -> 15 us  [run_local(): pl.pallas_call(functools.partial(local_kernel, pair, block, width, half),...]
    ppermute x19, starting transfers between devices: 33.5 us -> 27.7 us  [swap(): return lax.ppermute(x, 'seq', [(i, i ^ bit) for i in range(seq_count)])]
    slice x2 -> x0, local copies, waits for them, and re-layouts: 2.12 us -> none  [on_device(): grad[:, o * share:(o + 1) * share]]
    ppermute x3, starting transfers between devices: 8.55 us -> 6.55 us  [on_device(): lax.ppermute(squares, 'head', [(i, (i + s) % head_axis) for i in range(he...]
  transfers between devices with their start and end apart: 22 -> 22, of which waited for: 6 -> 6; matrix products, arithmetic and copies ran while one was open for 6% -> 4% of each run, Pallas kernels for 51% -> 44%
where the time goes in v2:
time: 101 us
  Pallas kernels  44.5 us (44%)
  starting transfers between devices  34.2 us (34%)
  waiting for transfers between devices  9.52 us (9%)
  other arithmetic  9.29 us (9%)
  local copies, waits for them, and re-layouts  2.8 us (3%)
    pallas_call x2, Pallas kernels, run_global(): pl.pallas_call(functools.partial(global_kernel, pair, units, block, width...  29.5 us
    ppermute x19, starting transfers between devices, swap(): return lax.ppermute(x, 'seq', [(i, i ^ bit) for i in range(seq_count)])  27.7 us
    pallas_call x2, Pallas kernels, run_local(): pl.pallas_call(functools.partial(local_kernel, pair, block, width, half),...  15 us
    ppermute x19, waiting for transfers between devices, swap(): return lax.ppermute(x, 'seq', [(i, i ^ bit) for i in range(seq_count)])  9.51 us
    ppermute x3, starting transfers between devices, on_device(): lax.ppermute(squares, 'head', [(i, (i + s) % head_axis) for i in range(he...  6.55 us
    convert_element_type x2, other arithmetic, away(): lax.dynamic_slice_in_dim(source, start, sizes[i] * width, 1).astype(F32)  4.01 us
    concatenate x4, other arithmetic, cat(): return jnp.concatenate(parts, axis)  2.36 us
  transfers between devices with their start and end apart: 22, of which 6 were waited for; matrix products, arithmetic and copies ran while one was open for 4% of the time, Pallas kernels for 44%

profile of v2, /device:TPU:0, one launch (start us, length us, event | category | flops | bytes accessed | tf_op | source)
XLA Modules:
  0.0 101.2 jit_solution(17060013024680064372)
XLA Ops:
  0.7 1.1 %constant_dynamic-slice_fusion = (bf16[256,128]{1,0:T(8,128)(2,1)S(1)}, bf16[256,128]{1,0:T(8,128)(2,1)S(1)}, bf16[256,128]{1,0:T(8,128)(2,1)S(1)}, bf16[256,128]{1,0:T(8,128)(2,1)S(1)}) fusion(bf16[256,256]{1,0:T(8,128)(2,1)} %param.8, s32[]{:T(128)S(6)} %select_n.69, s32[]{:T(128)S(6)} %select_n.66, bf16[256,256]{1,0:T(8,128)(2,1)} %param.7), kind=kLoop, calls=%fused_computation.21 | loop fusion | bytes 524296 | tf_op jit(solution)/shard_map/dynamic_slice | solution.py:295
  1.8 0.7 maximum_convert_fusion
  2.5 2.8 %dynamic-slice_convert_fusion.3 = (f32[256,1024]{1,0:T(8,128)}, f32[256,1024]{1,0:T(8,128)}) fusion(bf16[256,4096]{1,0:T(8,128)(2,1)} %refs_0_.3, s32[]{:T(128)S(6)} %select_n.67, s32[]{:T(128)S(6)} %select_n.72), kind=kLoop, calls=%fused_computation.5 | loop fusion | flops 524288 | bytes 3145736 | tf_op jit(solution)/shard_map/convert_element_type | solution.py:314
  6.2 2.6 %collective-permute-start.3 = (f32[1,256]{1,0:T(1,128)S(1)}, f32[1,256]{1,0:T(1,128)S(1)}, u32[]{:S(2)}, u32[]{:S(2)}) collective-permute-start(f32[1,256]{1,0:T(1,128)S(1)} %bitcast.5), channel_id=1, source_target_pairs={{0,1},{1,2},{2,3},{3,0},{4,5},{5,6},{6,7},{7,4},{8,9},{9,10},{10,1... | collective-permute-start | bytes 3080 | tf_op jit(solution)/shard_map/ppermute | solution.py:327
  8.9 2.6 %collective-permute-start.4 = (f32[1,256]{1,0:T(1,128)S(1)}, f32[1,256]{1,0:T(1,128)S(1)}, u32[]{:S(2)}, u32[]{:S(2)}) collective-permute-start(f32[1,256]{1,0:T(1,128)S(1)} %bitcast.6), channel_id=1, source_target_pairs={{0,2},{1,3},{2,0},{3,1},{4,6},{5,7},{6,4},{7,5},{8,10},{9,11},{10,... | collective-permute-start | bytes 3080 | tf_op jit(solution)/shard_map/ppermute | solution.py:327
  12.0 0.7 pad_add_fusion.pos_ref
  12.6 1.3 %dynamic-slice_convert_fusion.1 = (f32[256,1024]{1,0:T(8,128)}, f32[256,1024]{1,0:T(8,128)S(1)}) fusion(bf16[256,4096]{1,0:T(8,128)(2,1)S(1)} %copy-done, s32[]{:T(128)S(6)} %select_n.67, s32[]{:T(128)S(6)} %select_n.72), kind=kLoop, calls=%fused_computation.3 | loop fusion | flops 524288 | bytes 3145736 | tf_op jit(solution)/shard_map/convert_element_type | solution.py:314
  13.9 0.8 collective-permute-done.1
  14.7 1.3 %collective-permute-start.5 = (f32[1,256]{1,0:T(1,128)S(1)}, f32[1,256]{1,0:T(1,128)S(1)}, u32[]{:S(2)}, u32[]{:S(2)}) collective-permute-start(f32[1,256]{1,0:T(1,128)S(1)} %bitcast.7), channel_id=1, source_target_pairs={{0,3},{1,0},{2,1},{3,2},{4,7},{5,4},{6,5},{7,6},{8,11},{9,8},{10,9... | collective-permute-start | bytes 3080 | tf_op jit(solution)/shard_map/ppermute | solution.py:327
  16.1 0.9 pad_maximum_fusion.refs_4_
  17.0 1.5 %collective-permute-start.8 = (f32[256,256]{1,0:T(8,128)S(1)}, f32[256,256]{1,0:T(8,128)S(1)}, u32[]{:S(2)}, u32[]{:S(2)}) collective-permute-start(f32[256,256]{1,0:T(8,128)S(1)} %get-tuple-element.66.refs_11_), channel_id=1, source_target_pairs={{0,8},{4,12},{8,0},{12,4},{16,24},{20,28},{24,16},{28,20},{1,9},{5... | collective-permute-start | bytes 786440 | tf_op jit(solution)/shard_map/ppermute | solution.py:292
  18.5 1.5 %collective-permute-start.9 = (f32[256,256]{1,0:T(8,128)S(1)}, f32[256,256]{1,0:T(8,128)S(1)}, u32[]{:S(2)}, u32[]{:S(2)}) collective-permute-start(f32[256,256]{1,0:T(8,128)S(1)} %get-tuple-element.66.refs_11_), channel_id=1, source_target_pairs={{0,16},{4,20},{8,24},{12,28},{16,0},{20,4},{24,8},{28,12},{1,17},{... | collective-permute-start | bytes 786440 | tf_op jit(solution)/shard_map/ppermute | solution.py:292
  20.6 0.7 collective-permute-start.11
  21.3 7.6 %local_part.2 = (bf16[8,512,128]{2,1,0:T(8,128)(2,1)}, bf16[8,128,512]{2,1,0:T(8,128)(2,1)}, bf16[8,128,512]{2,1,0:T(8,128)(2,1)}, bf16[8,128,512]{2,1,0:T(8,128...) custom-call(s32[2]{0:T(128)} %pad_add_fusion.pos_ref, ...), custom_call_target="tpu_custom_call" | custom-call | flops 6144000000 | bytes 10000000 | tf_op jit(solution)/shard_map/local_part/pallas_call | solution.py:359
  29.6 1.2 %collective-permute-done.10.refs_14_ = f32[256,256]{1,0:T(8,128)} collective-permute-done((f32[256,256]{1,0:T(8,128)S(1)}, f32[256,256]{1,0:T(8,128)}, u32[]{:S(2)}, u32[]{:S(2)}) %collective-permute-start.10) | collective-permute-done | bytes 262176 | tf_op jit(solution)/shard_map/ppermute | solution.py:292
  30.8 1.2 %collective-permute-done.11.refs_16_ = f32[256,256]{1,0:T(8,128)} collective-permute-done((f32[256,256]{1,0:T(8,128)S(1)}, f32[256,256]{1,0:T(8,128)}, u32[]{:S(2)}, u32[]{:S(2)}) %collective-permute-start.11) | collective-permute-done | bytes 262176 | tf_op jit(solution)/shard_map/ppermute | solution.py:292
  32.0 1.5 %collective-permute-start.12 = (f32[256,256]{1,0:T(8,128)S(1)}, f32[256,256]{1,0:T(8,128)S(1)}, u32[]{:S(2)}, u32[]{:S(2)}) collective-permute-start(f32[256,256]{1,0:T(8,128)S(1)} %collective-permute-done.8.refs_13_), channel_id=1, source_target_pairs={{0,16},{4,20},{8,24},{12,28},{16,0},{20,4},{24,8},{28,12},{1,17},{... | collective-permute-start | bytes 786440 | tf_op jit(solution)/shard_map/ppermute | solution.py:292
  34.1 7.4 %local_part.3 = (bf16[8,512,128]{2,1,0:T(8,128)(2,1)}, bf16[8,128,512]{2,1,0:T(8,128)(2,1)}, bf16[8,128,512]{2,1,0:T(8,128)(2,1)}, bf16[8,128,512]{2,1,0:T(8,128...) custom-call(s32[2]{0:T(128)} %pad_add_fusion.pos_ref, ...), custom_call_target="tpu_custom_call" | custom-call | flops 6144000000 | bytes 10000000 | tf_op jit(solution)/shard_map/local_part/pallas_call | solution.py:359
  41.5 0.6 pad_maximum_fusion.4.refs_10_
  42.1 0.7 copy-done.8
  42.8 14.7 %global_part.2 = (f32[8,32,128]{2,1,0:T(8,128)}, f32[8,32,128]{2,1,0:T(8,128)}, f32[8,32,128]{2,1,0:T(8,128)}, f32[8,32,128]{2,1,0:T(8,128)}) custom-call(s32[2]{0:T(128)} %pad_add_fusion.pos_ref, bf16[8,512,128]{2,1,0:T(8,128)(2,1)} %get-tuple-element.49.refs_0_, bf16[8,128,512]{2,1,0:T(8,128)(2,1)} %get-tuple-element.50.refs_1_, ...), custom_call_target="tpu_custom_call" | custom-call | flops 12288000000 | bytes 10000000 | tf_op jit(solution)/shard_map/global_part/pallas_call | solution.py:400
  57.5 3.8 %collective-permute-start.14 = (f32[8,32,128]{2,1,0:T(8,128)}, f32[8,32,128]{2,1,0:T(8,128)S(1)}, u32[]{:S(2)}, u32[]{:S(2)}) collective-permute-start(f32[8,32,128]{2,1,0:T(8,128)} %get-tuple-element.75), channel_id=1, source_target_pairs={{0,8},{4,12},{8,0},{12,4},{16,24},{20,28},{24,16},{28,20},{1,9},{5... | collective-permute-start | bytes 393224 | tf_op jit(solution)/shard_map/ppermute | solution.py:292
  61.3 5.2 %collective-permute-start.15 = (f32[8,32,128]{2,1,0:T(8,128)}, f32[8,32,128]{2,1,0:T(8,128)S(1)}, u32[]{:S(2)}, u32[]{:S(2)}) collective-permute-start(f32[8,32,128]{2,1,0:T(8,128)} %get-tuple-element.76), channel_id=1, source_target_pairs={{0,16},{4,20},{8,24},{12,28},{16,0},{20,4},{24,8},{28,12},{1,17},{... | collective-permute-start | bytes 393224 | tf_op jit(solution)/shard_map/ppermute | solution.py:292
  66.5 1.0 copy-done.5
  67.5 14.8 %global_part.3 = (f32[8,32,128]{2,1,0:T(8,128)}, f32[8,32,128]{2,1,0:T(8,128)}, f32[8,32,128]{2,1,0:T(8,128)}, f32[8,32,128]{2,1,0:T(8,128)}) custom-call(s32[2]{0:T(128)} %pad_add_fusion.pos_ref, bf16[8,512,128]{2,1,0:T(8,128)(2,1)} %get-tuple-element.81.refs_0_, bf16[8,128,512]{2,1,0:T(8,128)(2,1)} %get-tuple-element.82.refs_1_, ...), custom_call_target="tpu_custom_call" | custom-call | flops 12288000000 | bytes 10000000 | tf_op jit(solution)/shard_map/global_part/pallas_call | solution.py:400
  82.4 10.0 %collective-permute-start.20 = (f32[8,32,128]{2,1,0:T(8,128)}, f32[8,32,128]{2,1,0:T(8,128)S(1)}, u32[]{:S(2)}, u32[]{:S(2)}) collective-permute-start(f32[8,32,128]{2,1,0:T(8,128)} %get-tuple-element.91), channel_id=1, source_target_pairs={{0,24},{4,28},{8,16},{12,20},{16,8},{20,12},{24,0},{28,4},{1,25},{... | collective-permute-start | bytes 393224 | tf_op jit(solution)/shard_map/ppermute | solution.py:292
  92.3 0.6 collective-permute-start.18
  93.0 3.9 %collective-permute-done.20 = f32[8,32,128]{2,1,0:T(8,128)S(1)} collective-permute-done((f32[8,32,128]{2,1,0:T(8,128)}, f32[8,32,128]{2,1,0:T(8,128)S(1)}, u32[]{:S(2)}, u32[]{:S(2)}) %collective-permute-start.20) | collective-permute-done | bytes 131104 | tf_op jit(solution)/shard_map/ppermute | solution.py:292
  96.9 1.0 collective-permute-done.19
  97.9 0.9 add_add_fusion
  99.0 1.3 %collective-permute-done.21 = f32[16,16,128]{2,1,0:T(8,128)S(1)} collective-permute-done((f32[16,16,128]{2,1,0:T(8,128)S(1)}, f32[16,16,128]{2,1,0:T(8,128)S(1)}, u32[]{:S(2)}, u32[]{:S(2)}) %collective-permute-start.21) | collective-permute-done | bytes 131104 | tf_op jit(solution)/shard_map/ppermute | solution.py:292
  100.3 0.9 pad_maximum_fusion.1
  (50 shorter events, 3.5 us)
Async XLA Ops:
  0.6 5.1 %copy-start = (bf16[256,4096]{1,0:T(8,128)(2,1)S(1)}, bf16[256,4096]{1,0:T(8,128)(2,1)}, u32[]{:S(2)}) copy-start(bf16[256,4096]{1,0:T(8,128)(2,1)} %refs_8_.3) | copy-start | bytes 6291460
  5.3 15.3 %collective-permute-start = (f32[256,1024]{1,0:T(8,128)}, f32[256,1024]{1,0:T(8,128)}, u32[]{:S(2)}, u32[]{:S(2)}) collective-permute-start(f32[256,1024]{1,0:T(8,128)} %get-tuple-element.94), channel_id=1, source_target_pairs={{0,4},{4,0},{8,12},{12,8},{16,20},{20,16},{24,28},{28,24},{1,5},{5... | collective-permute-start | bytes 3145736 | tf_op jit(solution)/shard_map/ppermute | solution.py:292
  6.2 10.8 %collective-permute-start.3 = (f32[1,256]{1,0:T(1,128)S(1)}, f32[1,256]{1,0:T(1,128)S(1)}, u32[]{:S(2)}, u32[]{:S(2)}) collective-permute-start(f32[1,256]{1,0:T(1,128)S(1)} %bitcast.5), channel_id=1, source_target_pairs={{0,1},{1,2},{2,3},{3,0},{4,5},{5,6},{6,7},{7,4},{8,9},{9,10},{10,1... | collective-permute-start | bytes 3080 | tf_op jit(solution)/shard_map/ppermute | solution.py:327
  8.9 9.7 %collective-permute-start.4 = (f32[1,256]{1,0:T(1,128)S(1)}, f32[1,256]{1,0:T(1,128)S(1)}, u32[]{:S(2)}, u32[]{:S(2)}) collective-permute-start(f32[1,256]{1,0:T(1,128)S(1)} %bitcast.6), channel_id=1, source_target_pairs={{0,2},{1,3},{2,0},{3,1},{4,6},{5,7},{6,4},{7,5},{8,10},{9,11},{10,... | collective-permute-start | bytes 3080 | tf_op jit(solution)/shard_map/ppermute | solution.py:327
  11.4 22.1 %collective-permute-start.7 = (f32[256,1024]{1,0:T(8,128)}, f32[256,1024]{1,0:T(8,128)}, u32[]{:S(2)}, u32[]{:S(2)}) collective-permute-start(f32[256,1024]{1,0:T(8,128)} %get-tuple-element.95), channel_id=1, source_target_pairs={{0,4},{4,0},{8,12},{12,8},{16,20},{20,16},{24,28},{28,24},{1,5},{5... | collective-permute-start | bytes 3145736 | tf_op jit(solution)/shard_map/ppermute | solution.py:292
  11.4 3.2 %collective-permute-start.1 = (f32[256,256]{1,0:T(8,128)}, f32[256,256]{1,0:T(8,128)S(1)}, u32[]{:S(2)}, u32[]{:S(2)}) collective-permute-start(f32[256,256]{1,0:T(8,128)} %maximum_convert_fusion), channel_id=1, source_target_pairs={{0,4},{4,0},{8,12},{12,8},{16,20},{20,16},{24,28},{28,24},{1,5},{5... | collective-permute-start | bytes 786440 | tf_op jit(solution)/shard_map/ppermute | solution.py:292
  14.7 5.3 %collective-permute-start.5 = (f32[1,256]{1,0:T(1,128)S(1)}, f32[1,256]{1,0:T(1,128)S(1)}, u32[]{:S(2)}, u32[]{:S(2)}) collective-permute-start(f32[1,256]{1,0:T(1,128)S(1)} %bitcast.7), channel_id=1, source_target_pairs={{0,3},{1,0},{2,1},{3,2},{4,7},{5,4},{6,5},{7,6},{8,11},{9,8},{10,9... | collective-permute-start | bytes 3080 | tf_op jit(solution)/shard_map/ppermute | solution.py:327
  16.1 12.8 %copy-start.2 = (f32[256,256]{1,0:T(8,128)}, f32[256,256]{1,0:T(8,128)S(1)}, u32[]{:S(2)}) copy-start(f32[256,256]{1,0:T(8,128)S(1)} %get-tuple-element.66.refs_11_) | copy-start | bytes 786436
  16.1 12.8 %copy-start.3 = (f32[256,256]{1,0:T(8,128)}, f32[256,256]{1,0:T(8,128)S(1)}, u32[]{:S(2)}) copy-start(f32[256,256]{1,0:T(8,128)S(1)} %get-tuple-element.67.refs_12_) | copy-start | bytes 786436
  17.0 11.9 %collective-permute-start.8 = (f32[256,256]{1,0:T(8,128)S(1)}, f32[256,256]{1,0:T(8,128)S(1)}, u32[]{:S(2)}, u32[]{:S(2)}) collective-permute-start(f32[256,256]{1,0:T(8,128)S(1)} %get-tuple-element.66.refs_11_), channel_id=1, source_target_pairs={{0,8},{4,12},{8,0},{12,4},{16,24},{20,28},{24,16},{28,20},{1,9},{5... | collective-permute-start | bytes 786440 | tf_op jit(solution)/shard_map/ppermute | solution.py:292
  18.5 10.5 %collective-permute-start.9 = (f32[256,256]{1,0:T(8,128)S(1)}, f32[256,256]{1,0:T(8,128)S(1)}, u32[]{:S(2)}, u32[]{:S(2)}) collective-permute-start(f32[256,256]{1,0:T(8,128)S(1)} %get-tuple-element.66.refs_11_), channel_id=1, source_target_pairs={{0,16},{4,20},{8,24},{12,28},{16,0},{20,4},{24,8},{28,12},{1,17},{... | collective-permute-start | bytes 786440 | tf_op jit(solution)/shard_map/ppermute | solution.py:292
  20.0 10.8 %collective-permute-start.10 = (f32[256,256]{1,0:T(8,128)S(1)}, f32[256,256]{1,0:T(8,128)}, u32[]{:S(2)}, u32[]{:S(2)}) collective-permute-start(f32[256,256]{1,0:T(8,128)S(1)} %get-tuple-element.67.refs_12_), channel_id=1, source_target_pairs={{0,8},{4,12},{8,0},{12,4},{16,24},{20,28},{24,16},{28,20},{1,9},{5... | collective-permute-start | bytes 786440 | tf_op jit(solution)/shard_map/ppermute | solution.py:292
  20.6 11.4 %collective-permute-start.11 = (f32[256,256]{1,0:T(8,128)S(1)}, f32[256,256]{1,0:T(8,128)}, u32[]{:S(2)}, u32[]{:S(2)}) collective-permute-start(f32[256,256]{1,0:T(8,128)S(1)} %get-tuple-element.67.refs_12_), channel_id=1, source_target_pairs={{0,16},{4,20},{8,24},{12,28},{16,0},{20,4},{24,8},{28,12},{1,17},{... | collective-permute-start | bytes 786440 | tf_op jit(solution)/shard_map/ppermute | solution.py:292
  21.3 7.6 %copy-start.1 = (f32[256,1024]{1,0:T(8,128)S(1)}, f32[256,1024]{1,0:T(8,128)}, u32[]{:S(2)}) copy-start(f32[256,1024]{1,0:T(8,128)} %get-tuple-element.92) | copy-start | bytes 3145732
  28.9 12.6 %copy-start.6 = (f32[256,256]{1,0:T(8,128)}, f32[256,256]{1,0:T(8,128)S(1)}, u32[]{:S(2)}) copy-start(f32[256,256]{1,0:T(8,128)S(1)} %collective-permute-done.8.refs_13_) | copy-start | bytes 786436
  28.9 13.2 %collective-permute-start.2 = (f32[256,1024]{1,0:T(8,128)S(1)}, f32[256,1024]{1,0:T(8,128)}, u32[]{:S(2)}, u32[]{:S(2)}) collective-permute-start(f32[256,1024]{1,0:T(8,128)S(1)} %copy-done.1), channel_id=1, source_target_pairs={{0,4},{4,0},{8,12},{12,8},{16,20},{20,16},{24,28},{28,24},{1,5},{5... | collective-permute-start | bytes 3145736 | tf_op jit(solution)/shard_map/ppermute | solution.py:292
  29.0 12.5 %copy-start.7 = (f32[256,256]{1,0:T(8,128)}, f32[256,256]{1,0:T(8,128)S(1)}, u32[]{:S(2)}) copy-start(f32[256,256]{1,0:T(8,128)S(1)} %collective-permute-done.9.refs_15_) | copy-start | bytes 786436
  29.0 37.5 %collective-permute-start.17 = (f32[256,1024]{1,0:T(8,128)S(1)}, f32[256,1024]{1,0:T(8,128)S(1)}, u32[]{:S(2)}, u32[]{:S(2)}) collective-permute-start(f32[256,1024]{1,0:T(8,128)S(1)} %get-tuple-element.93), channel_id=1, source_target_pairs={{0,4},{4,0},{8,12},{12,8},{16,20},{20,16},{24,28},{28,24},{1,5},{5... | collective-permute-start | bytes 3145736 | tf_op jit(solution)/shard_map/ppermute | solution.py:292
  30.8 10.7 %collective-permute-start.6 = (f32[1,256]{1,0:T(1,128)S(1)}, f32[1,256]{1,0:T(1,128)S(1)}, u32[]{:S(2)}, u32[]{:S(2)}) collective-permute-start(f32[1,256]{1,0:T(1,128)S(1)} %add_divide_fusion), channel_id=1, source_target_pairs={{0,4},{4,0},{8,12},{12,8},{16,20},{20,16},{24,28},{28,24},{1,5},{5... | collective-permute-start | bytes 3080 | tf_op jit(solution)/shard_map/ppermute | solution.py:292
  32.0 10.1 %collective-permute-start.12 = (f32[256,256]{1,0:T(8,128)S(1)}, f32[256,256]{1,0:T(8,128)S(1)}, u32[]{:S(2)}, u32[]{:S(2)}) collective-permute-start(f32[256,256]{1,0:T(8,128)S(1)} %collective-permute-done.8.refs_13_), channel_id=1, source_target_pairs={{0,16},{4,20},{8,24},{12,28},{16,0},{20,4},{24,8},{28,12},{1,17},{... | collective-permute-start | bytes 786440 | tf_op jit(solution)/shard_map/ppermute | solution.py:292
  33.5 8.6 %collective-permute-start.13 = (f32[256,256]{1,0:T(8,128)}, f32[256,256]{1,0:T(8,128)}, u32[]{:S(2)}, u32[]{:S(2)}) collective-permute-start(f32[256,256]{1,0:T(8,128)} %collective-permute-done.11.refs_16_), channel_id=1, source_target_pairs={{0,8},{4,12},{8,0},{12,4},{16,24},{20,28},{24,16},{28,20},{1,9},{5... | collective-permute-start | bytes 786440 | tf_op jit(solution)/shard_map/ppermute | solution.py:292
  42.1 0.7 copy-start.8
  57.5 34.9 %collective-permute-start.14 = (f32[8,32,128]{2,1,0:T(8,128)}, f32[8,32,128]{2,1,0:T(8,128)S(1)}, u32[]{:S(2)}, u32[]{:S(2)}) collective-permute-start(f32[8,32,128]{2,1,0:T(8,128)} %get-tuple-element.75), channel_id=1, source_target_pairs={{0,8},{4,12},{8,0},{12,4},{16,24},{20,28},{24,16},{28,20},{1,9},{5... | collective-permute-start | bytes 393224 | tf_op jit(solution)/shard_map/ppermute | solution.py:292
  61.3 31.7 %collective-permute-start.15 = (f32[8,32,128]{2,1,0:T(8,128)}, f32[8,32,128]{2,1,0:T(8,128)S(1)}, u32[]{:S(2)}, u32[]{:S(2)}) collective-permute-start(f32[8,32,128]{2,1,0:T(8,128)} %get-tuple-element.76), channel_id=1, source_target_pairs={{0,16},{4,20},{8,24},{12,28},{16,0},{20,4},{24,8},{28,12},{1,17},{... | collective-permute-start | bytes 393224 | tf_op jit(solution)/shard_map/ppermute | solution.py:292
  66.5 26.5 %collective-permute-start.16 = (f32[8,32,128]{2,1,0:T(8,128)}, f32[8,32,128]{2,1,0:T(8,128)S(1)}, u32[]{:S(2)}, u32[]{:S(2)}) collective-permute-start(f32[8,32,128]{2,1,0:T(8,128)} %get-tuple-element.77), channel_id=1, source_target_pairs={{0,24},{4,28},{8,16},{12,20},{16,8},{20,12},{24,0},{28,4},{1,25},{... | collective-permute-start | bytes 393224 | tf_op jit(solution)/shard_map/ppermute | solution.py:292
  66.5 1.0 copy-start.5
  67.5 25.5 %copy-start.4 = (f32[8,32,128]{2,1,0:T(8,128)S(1)}, f32[8,32,128]{2,1,0:T(8,128)}, u32[]{:S(2)}) copy-start(f32[8,32,128]{2,1,0:T(8,128)} %get-tuple-element.74) | copy-start | bytes 393220
  82.4 14.5 %collective-permute-start.20 = (f32[8,32,128]{2,1,0:T(8,128)}, f32[8,32,128]{2,1,0:T(8,128)S(1)}, u32[]{:S(2)}, u32[]{:S(2)}) collective-permute-start(f32[8,32,128]{2,1,0:T(8,128)} %get-tuple-element.91), channel_id=1, source_target_pairs={{0,24},{4,28},{8,16},{12,20},{16,8},{20,12},{24,0},{28,4},{1,25},{... | collective-permute-start | bytes 393224 | tf_op jit(solution)/shard_map/ppermute | solution.py:292
  92.3 5.6 %collective-permute-start.19 = (f32[8,32,128]{2,1,0:T(8,128)}, f32[8,32,128]{2,1,0:T(8,128)S(1)}, u32[]{:S(2)}, u32[]{:S(2)}) collective-permute-start(f32[8,32,128]{2,1,0:T(8,128)} %get-tuple-element.90), channel_id=1, source_target_pairs={{0,16},{4,20},{8,24},{12,28},{16,0},{20,4},{24,8},{28,12},{1,17},{... | collective-permute-start | bytes 393224 | tf_op jit(solution)/shard_map/ppermute | solution.py:292
  92.3 5.6 %collective-permute-start.18 = (f32[8,32,128]{2,1,0:T(8,128)}, f32[8,32,128]{2,1,0:T(8,128)S(1)}, u32[]{:S(2)}, u32[]{:S(2)}) collective-permute-start(f32[8,32,128]{2,1,0:T(8,128)} %get-tuple-element.89), channel_id=1, source_target_pairs={{0,8},{4,12},{8,0},{12,4},{16,24},{20,28},{24,16},{28,20},{1,9},{5... | collective-permute-start | bytes 393224 | tf_op jit(solution)/shard_map/ppermute | solution.py:292
  98.9 1.4 %collective-permute-start.21 = (f32[16,16,128]{2,1,0:T(8,128)S(1)}, f32[16,16,128]{2,1,0:T(8,128)S(1)}, u32[]{:S(2)}, u32[]{:S(2)}) collective-permute-start(f32[16,16,128]{2,1,0:T(8,128)S(1)} %pad_maximum_fusion.2), channel_id=1, source_target_pairs={{0,4},{4,0},{8,12},{12,8},{16,20},{20,16},{24,28},{28,24},{1,5},{5... | collective-permute-start | bytes 393224 | tf_op jit(solution)/shard_map/ppermute | solution.py:292
